TPU v7x, 256 devices: a whole 4x4x8 slice. The times are simulated.
256 devices in a mesh: rep: 32 (over z, y), data: 8 (over x, core).
Axes of the slice: x: 4, y: 4, z: 8, core: 2. Of those that a mesh axis runs over, the one named last changes fastest.
Arguments:
- img_feat: bfloat16 [196608, 1024], P(('rep', 'data'))
- txt_feat: bfloat16 [196608, 1024], P(('rep', 'data'))
- w_img: bfloat16 [1024, 1024], replicated
- w_txt: bfloat16 [1024, 1024], replicated
- log_temp: float32 [], replicated
- logit_bias: float32 [], replicated
Outputs:
- output 1: float32 [], replicated
- output 2: float32 [], replicated
- output 3: float32 [], replicated
- output 4: float32 [1024, 1024], replicated
- output 5: float32 [1024, 1024], replicated
All inputs are finite; a program needn't handle non-finite values.
Results may differ from a plain program's by a relative error of at most 0.001.
Values are sent between devices in bfloat16 or wider.
A program may use at most 768 MiB of HBM per device.

v0:
```python
import jax
import jax.numpy as jnp
from jax import lax
from jax.sharding import PartitionSpec as P


def normalize_rows(raw_emb):
    inv_norm = lax.rsqrt(jnp.sum(raw_emb * raw_emb, axis=1, keepdims=True))
    return raw_emb * inv_norm, inv_norm


def backward_norm(grad_unit, unit_emb, inv_norm):
    proj = jnp.sum(unit_emb * grad_unit, axis=1, keepdims=True)
    return (inv_norm * (grad_unit - unit_emb * proj)).astype(jnp.bfloat16)


def contract_rows(left, right):
    return lax.dot_general(left, right, (((0,), (0,)), ((), ())), preferred_element_type=jnp.float32)


def tile_terms(img_emb, txt_blk, temp_scale, logit_bias, row_offset, total_rows):
    tile_dots = lax.dot_general(img_emb, txt_blk, (((1,), (1,)), ((), ())), preferred_element_type=jnp.float32)
    row_ids = row_offset + jnp.arange(img_emb.shape[0])[:, None]
    col_ids = jnp.arange(txt_blk.shape[0])[None, :]
    sign_mat = jnp.where(row_ids == col_ids, 1.0, -1.0)
    margin = sign_mat * (temp_scale * tile_dots + logit_bias)
    grad_z = -sign_mat * jax.nn.sigmoid(-margin) / total_rows
    scal_part = jnp.stack([jnp.sum(jax.nn.softplus(-margin)), temp_scale * jnp.sum(grad_z * tile_dots), jnp.sum(grad_z)])
    h_mat = (temp_scale * grad_z).astype(jnp.bfloat16)
    img_part = jnp.dot(h_mat, txt_blk, preferred_element_type=jnp.float32)
    txt_part = contract_rows(h_mat, img_emb)
    return img_part, txt_part, scal_part


def solution(mesh):
    data_n = mesh.shape['data']
    rep_n = mesh.shape['rep']
    shift_perm = [(src_dev, (src_dev + 1) % data_n) for src_dev in range(data_n)]
    row_spec = P(('rep', 'data'), None)

    def device_body(img_loc, txt_loc, w_img, w_txt, log_temp, logit_bias):
        rows_n = img_loc.shape[0]
        total_rows = rows_n * rep_n * data_n
        temp_scale = jnp.exp(log_temp)
        unit_img, inv_img = normalize_rows(jnp.dot(img_loc, w_img, preferred_element_type=jnp.float32))
        unit_txt, inv_txt = normalize_rows(jnp.dot(txt_loc, w_txt, preferred_element_type=jnp.float32))
        emb_img = unit_img.astype(jnp.bfloat16)
        emb_txt = unit_txt.astype(jnp.bfloat16)
        home_img, home_txt, home_scal = tile_terms(emb_img, emb_txt, temp_scale, logit_bias, 0, total_rows)

        def visit_step(step_idx, loop_state):
            txt_blk, txt_acc, img_acc, scal_acc = loop_state
            txt_blk = lax.ppermute(txt_blk, 'data', shift_perm)
            txt_acc = lax.ppermute(txt_acc, 'data', shift_perm)
            img_part, txt_part, scal_part = tile_terms(emb_img, txt_blk, temp_scale, logit_bias, rows_n, total_rows)
            return (txt_blk, txt_acc + txt_part, img_acc + img_part, scal_acc + scal_part)

        final_state = lax.fori_loop(1, data_n, visit_step, (emb_txt, home_txt, home_img, home_scal))
        txt_grad = lax.ppermute(final_state[1], 'data', shift_perm)
        img_grad = final_state[2]
        dw_img = contract_rows(img_loc, backward_norm(img_grad, unit_img, inv_img))
        dw_txt = contract_rows(txt_loc, backward_norm(txt_grad, unit_txt, inv_txt))
        dw_img, dw_txt, scal_sum = lax.psum((dw_img, dw_txt, final_state[3]), ('rep', 'data'))
        return scal_sum[0] / total_rows, scal_sum[1], scal_sum[2], dw_img, dw_txt

    return jax.shard_map(device_body, mesh=mesh, in_specs=(row_spec, row_spec, P(), P(), P(), P()), out_specs=(P(), P(), P(), P(), P()), check_vma=False)
```

profile of v0, /device:TPU:1, one launch (start us, length us, event | category | flops | bytes accessed | tf_op | source)
XLA Modules:
  0.0 802.4 jit_solution(2939413725773584085)
XLA Ops:
  33.2 418.4 %while.17 = (s32[]{:T(128)}, bf16[768,1024]{1,0:T(8,128)(2,1)}, f32[768,1024]{1,0:T(8,128)}, f32[768,1024]{1,0:T(8,128)}, f32[3]{0:T(128)S(1)}, /*index=5*/f32[]...) while((s32[]{:T(128)}, bf16[768,1024]{1,0:T(8,128)(2,1)}, f32[768,1024]{1,0:T(8,128)}, ...), condition=%wide.region_9.10_spmd, body=%wide.region_5.9_spmd.sunk | while | flops 3650814720 | bytes 88879480 | solution.py:58
  36.0 17.3 %collective-permute-done = bf16[768,1024]{1,0:T(8,128)(2,1)} collective-permute-done((bf16[768,1024]{1,0:T(8,128)(2,1)}, bf16[768,1024]{1,0:T(8,128)(2,1)}, u32[]{:S(2)}, u32[]{:S(2)}) %collective-permute-start) | collective-permute-done | bytes 1572896 | tf_op jit(solution)/shard_map/while/body/eval_jaxpr/ppermute | solution.py:53
  53.3 7.9 fusion.38
  71.5 15.5 %collective-permute-done.1 = f32[768,1024]{1,0:T(8,128)} collective-permute-done((f32[768,1024]{1,0:T(8,128)}, f32[768,1024]{1,0:T(8,128)}, u32[]{:S(2)}, u32[]{:S(2)}) %collective-permute-start.1) | collective-permute-done | bytes 3145760 | tf_op jit(solution)/shard_map/while/body/eval_jaxpr/ppermute | solution.py:54
  95.7 17.3 %collective-permute-done = bf16[768,1024]{1,0:T(8,128)(2,1)} collective-permute-done((bf16[768,1024]{1,0:T(8,128)(2,1)}, bf16[768,1024]{1,0:T(8,128)(2,1)}, u32[]{:S(2)}, u32[]{:S(2)}) %collective-permute-start) | collective-permute-done | bytes 1572896 | tf_op jit(solution)/shard_map/while/body/eval_jaxpr/ppermute | solution.py:53
  113.0 7.9 fusion.38
  131.2 15.5 %collective-permute-done.1 = f32[768,1024]{1,0:T(8,128)} collective-permute-done((f32[768,1024]{1,0:T(8,128)}, f32[768,1024]{1,0:T(8,128)}, u32[]{:S(2)}, u32[]{:S(2)}) %collective-permute-start.1) | collective-permute-done | bytes 3145760 | tf_op jit(solution)/shard_map/while/body/eval_jaxpr/ppermute | solution.py:54
  155.4 17.3 %collective-permute-done = bf16[768,1024]{1,0:T(8,128)(2,1)} collective-permute-done((bf16[768,1024]{1,0:T(8,128)(2,1)}, bf16[768,1024]{1,0:T(8,128)(2,1)}, u32[]{:S(2)}, u32[]{:S(2)}) %collective-permute-start) | collective-permute-done | bytes 1572896 | tf_op jit(solution)/shard_map/while/body/eval_jaxpr/ppermute | solution.py:53
  172.8 7.9 fusion.38
  191.0 15.5 %collective-permute-done.1 = f32[768,1024]{1,0:T(8,128)} collective-permute-done((f32[768,1024]{1,0:T(8,128)}, f32[768,1024]{1,0:T(8,128)}, u32[]{:S(2)}, u32[]{:S(2)}) %collective-permute-start.1) | collective-permute-done | bytes 3145760 | tf_op jit(solution)/shard_map/while/body/eval_jaxpr/ppermute | solution.py:54
  215.2 17.3 %collective-permute-done = bf16[768,1024]{1,0:T(8,128)(2,1)} collective-permute-done((bf16[768,1024]{1,0:T(8,128)(2,1)}, bf16[768,1024]{1,0:T(8,128)(2,1)}, u32[]{:S(2)}, u32[]{:S(2)}) %collective-permute-start) | collective-permute-done | bytes 1572896 | tf_op jit(solution)/shard_map/while/body/eval_jaxpr/ppermute | solution.py:53
  232.5 7.9 fusion.38
  250.7 15.5 %collective-permute-done.1 = f32[768,1024]{1,0:T(8,128)} collective-permute-done((f32[768,1024]{1,0:T(8,128)}, f32[768,1024]{1,0:T(8,128)}, u32[]{:S(2)}, u32[]{:S(2)}) %collective-permute-start.1) | collective-permute-done | bytes 3145760 | tf_op jit(solution)/shard_map/while/body/eval_jaxpr/ppermute | solution.py:54
  274.9 17.3 %collective-permute-done = bf16[768,1024]{1,0:T(8,128)(2,1)} collective-permute-done((bf16[768,1024]{1,0:T(8,128)(2,1)}, bf16[768,1024]{1,0:T(8,128)(2,1)}, u32[]{:S(2)}, u32[]{:S(2)}) %collective-permute-start) | collective-permute-done | bytes 1572896 | tf_op jit(solution)/shard_map/while/body/eval_jaxpr/ppermute | solution.py:53
  292.2 7.9 fusion.38
  310.4 15.5 %collective-permute-done.1 = f32[768,1024]{1,0:T(8,128)} collective-permute-done((f32[768,1024]{1,0:T(8,128)}, f32[768,1024]{1,0:T(8,128)}, u32[]{:S(2)}, u32[]{:S(2)}) %collective-permute-start.1) | collective-permute-done | bytes 3145760 | tf_op jit(solution)/shard_map/while/body/eval_jaxpr/ppermute | solution.py:54
  334.7 17.3 %collective-permute-done = bf16[768,1024]{1,0:T(8,128)(2,1)} collective-permute-done((bf16[768,1024]{1,0:T(8,128)(2,1)}, bf16[768,1024]{1,0:T(8,128)(2,1)}, u32[]{:S(2)}, u32[]{:S(2)}) %collective-permute-start) | collective-permute-done | bytes 1572896 | tf_op jit(solution)/shard_map/while/body/eval_jaxpr/ppermute | solution.py:53
  352.0 7.9 fusion.38
  370.2 15.5 %collective-permute-done.1 = f32[768,1024]{1,0:T(8,128)} collective-permute-done((f32[768,1024]{1,0:T(8,128)}, f32[768,1024]{1,0:T(8,128)}, u32[]{:S(2)}, u32[]{:S(2)}) %collective-permute-start.1) | collective-permute-done | bytes 3145760 | tf_op jit(solution)/shard_map/while/body/eval_jaxpr/ppermute | solution.py:54
  394.4 17.3 %collective-permute-done = bf16[768,1024]{1,0:T(8,128)(2,1)} collective-permute-done((bf16[768,1024]{1,0:T(8,128)(2,1)}, bf16[768,1024]{1,0:T(8,128)(2,1)}, u32[]{:S(2)}, u32[]{:S(2)}) %collective-permute-start) | collective-permute-done | bytes 1572896 | tf_op jit(solution)/shard_map/while/body/eval_jaxpr/ppermute | solution.py:53
  429.9 15.5 %collective-permute-done.1 = f32[768,1024]{1,0:T(8,128)} collective-permute-done((f32[768,1024]{1,0:T(8,128)}, f32[768,1024]{1,0:T(8,128)}, u32[]{:S(2)}, u32[]{:S(2)}) %collective-permute-start.1) | collective-permute-done | bytes 3145760 | tf_op jit(solution)/shard_map/while/body/eval_jaxpr/ppermute | solution.py:54
  464.7 23.6 %collective-permute-done.2 = f32[768,1024]{1,0:T(8,128)S(1)} collective-permute-done((f32[768,1024]{1,0:T(8,128)}, f32[768,1024]{1,0:T(8,128)S(1)}, u32[]{:S(2)}, u32[]{:S(2)}) %collective-permute-start.2) | collective-permute-done | bytes 3145760 | tf_op jit(solution)/shard_map/ppermute | solution.py:59
  493.1 89.4 %psum.21 = f32[3]{0:T(128)S(1)} all-reduce(f32[3]{0:T(128)S(1)} %get-tuple-element.86), channel_id=1, replica_groups=mesh['rep'=32,'data'=8] {'rep','data'}, use_global_device_ids=true, to_apply=%region_10.11 | all-reduce | flops 3 | bytes 24 | tf_op jit(solution)/shard_map/psum | solution.py:63
  583.7 200.1 %all-reduce.3.cloned.1.call-done = (f32[1024,1024]{0,1:T(8,128)}, f32[1024,1024]{0,1:T(8,128)}) async-done(((f32[1024,1024]{0,1:T(8,128)}, f32[1024,1024]{0,1:T(8,128)}), (f32[1024,1024]{0,1:T(8,128)}, f32[1024,1024]{0,1:T(8,128)})) %all-reduce.3.cloned.1.call-update) | async-done | bytes 8388624 | tf_op jit(solution)/shard_map/psum | solution.py:63
  (151 shorter events, 189.0 us)
Async XLA Ops:
  7.2 776.6 %all-reduce.3.cloned.1.call-start = ((), (), s32[]{:S(2)}) async-start(), calls=%async_computation | async-start | bytes 16777216 | tf_op jit(solution)/shard_map/psum | solution.py:63
  33.2 420.9 %copy-start.14 = (f32[768]{0:T(1024)S(1)}, f32[768]{0:T(1024)}, u32[]{:S(2)}) copy-start(f32[768]{0:T(1024)} %copy-done.13) | copy-start | bytes 9220
  33.3 20.0 %collective-permute-start = (bf16[768,1024]{1,0:T(8,128)(2,1)}, bf16[768,1024]{1,0:T(8,128)(2,1)}, u32[]{:S(2)}, u32[]{:S(2)}) collective-permute-start(bf16[768,1024]{1,0:T(8,128)(2,1)} %get-tuple-element.205), channel_id=1, source_target_pairs={{0,1},{1,2},{2,3},{3,4},{4,5},{5,6},{6,7},{7,0},{8,9},{9,10},{10,1... | collective-permute-start | bytes 4718600 | tf_op jit(solution)/shard_map/while/body/eval_jaxpr/ppermute | solution.py:53
  35.9 51.0 %collective-permute-start.1 = (f32[768,1024]{1,0:T(8,128)}, f32[768,1024]{1,0:T(8,128)}, u32[]{:S(2)}, u32[]{:S(2)}) collective-permute-start(f32[768,1024]{1,0:T(8,128)} %get-tuple-element.206), channel_id=1, source_target_pairs={{0,1},{1,2},{2,3},{3,4},{4,5},{5,6},{6,7},{7,0},{8,9},{9,10},{10,1... | collective-permute-start | bytes 9437192 | tf_op jit(solution)/shard_map/while/body/eval_jaxpr/ppermute | solution.py:54
  71.5 21.7 %copy-start.4 = (f32[768,1024]{1,0:T(8,128)}, f32[768,1024]{1,0:T(8,128)S(1)}, u32[]{:S(2)}) copy-start(f32[768,1024]{1,0:T(8,128)S(1)} %convolution_add_fusion.5) | copy-start | bytes 9437188 | tf_op jit(solution)/shard_map/while
  93.2 19.8 %collective-permute-start = (bf16[768,1024]{1,0:T(8,128)(2,1)}, bf16[768,1024]{1,0:T(8,128)(2,1)}, u32[]{:S(2)}, u32[]{:S(2)}) collective-permute-start(bf16[768,1024]{1,0:T(8,128)(2,1)} %get-tuple-element.205), channel_id=1, source_target_pairs={{0,1},{1,2},{2,3},{3,4},{4,5},{5,6},{6,7},{7,0},{8,9},{9,10},{10,1... | collective-permute-start | bytes 4718600 | tf_op jit(solution)/shard_map/while/body/eval_jaxpr/ppermute | solution.py:53
  95.7 51.0 %collective-permute-start.1 = (f32[768,1024]{1,0:T(8,128)}, f32[768,1024]{1,0:T(8,128)}, u32[]{:S(2)}, u32[]{:S(2)}) collective-permute-start(f32[768,1024]{1,0:T(8,128)} %get-tuple-element.206), channel_id=1, source_target_pairs={{0,1},{1,2},{2,3},{3,4},{4,5},{5,6},{6,7},{7,0},{8,9},{9,10},{10,1... | collective-permute-start | bytes 9437192 | tf_op jit(solution)/shard_map/while/body/eval_jaxpr/ppermute | solution.py:54
  131.2 21.7 %copy-start.4 = (f32[768,1024]{1,0:T(8,128)}, f32[768,1024]{1,0:T(8,128)S(1)}, u32[]{:S(2)}) copy-start(f32[768,1024]{1,0:T(8,128)S(1)} %convolution_add_fusion.5) | copy-start | bytes 9437188 | tf_op jit(solution)/shard_map/while
  152.9 19.8 %collective-permute-start = (bf16[768,1024]{1,0:T(8,128)(2,1)}, bf16[768,1024]{1,0:T(8,128)(2,1)}, u32[]{:S(2)}, u32[]{:S(2)}) collective-permute-start(bf16[768,1024]{1,0:T(8,128)(2,1)} %get-tuple-element.205), channel_id=1, source_target_pairs={{0,1},{1,2},{2,3},{3,4},{4,5},{5,6},{6,7},{7,0},{8,9},{9,10},{10,1... | collective-permute-start | bytes 4718600 | tf_op jit(solution)/shard_map/while/body/eval_jaxpr/ppermute | solution.py:53
  155.4 51.0 %collective-permute-start.1 = (f32[768,1024]{1,0:T(8,128)}, f32[768,1024]{1,0:T(8,128)}, u32[]{:S(2)}, u32[]{:S(2)}) collective-permute-start(f32[768,1024]{1,0:T(8,128)} %get-tuple-element.206), channel_id=1, source_target_pairs={{0,1},{1,2},{2,3},{3,4},{4,5},{5,6},{6,7},{7,0},{8,9},{9,10},{10,1... | collective-permute-start | bytes 9437192 | tf_op jit(solution)/shard_map/while/body/eval_jaxpr/ppermute | solution.py:54
  212.7 19.8 %collective-permute-start = (bf16[768,1024]{1,0:T(8,128)(2,1)}, bf16[768,1024]{1,0:T(8,128)(2,1)}, u32[]{:S(2)}, u32[]{:S(2)}) collective-permute-start(bf16[768,1024]{1,0:T(8,128)(2,1)} %get-tuple-element.205), channel_id=1, source_target_pairs={{0,1},{1,2},{2,3},{3,4},{4,5},{5,6},{6,7},{7,0},{8,9},{9,10},{10,1... | collective-permute-start | bytes 4718600 | tf_op jit(solution)/shard_map/while/body/eval_jaxpr/ppermute | solution.py:53
  215.2 51.0 %collective-permute-start.1 = (f32[768,1024]{1,0:T(8,128)}, f32[768,1024]{1,0:T(8,128)}, u32[]{:S(2)}, u32[]{:S(2)}) collective-permute-start(f32[768,1024]{1,0:T(8,128)} %get-tuple-element.206), channel_id=1, source_target_pairs={{0,1},{1,2},{2,3},{3,4},{4,5},{5,6},{6,7},{7,0},{8,9},{9,10},{10,1... | collective-permute-start | bytes 9437192 | tf_op jit(solution)/shard_map/while/body/eval_jaxpr/ppermute | solution.py:54
  250.7 21.7 %copy-start.4 = (f32[768,1024]{1,0:T(8,128)}, f32[768,1024]{1,0:T(8,128)S(1)}, u32[]{:S(2)}) copy-start(f32[768,1024]{1,0:T(8,128)S(1)} %convolution_add_fusion.5) | copy-start | bytes 9437188 | tf_op jit(solution)/shard_map/while
  272.4 19.8 %collective-permute-start = (bf16[768,1024]{1,0:T(8,128)(2,1)}, bf16[768,1024]{1,0:T(8,128)(2,1)}, u32[]{:S(2)}, u32[]{:S(2)}) collective-permute-start(bf16[768,1024]{1,0:T(8,128)(2,1)} %get-tuple-element.205), channel_id=1, source_target_pairs={{0,1},{1,2},{2,3},{3,4},{4,5},{5,6},{6,7},{7,0},{8,9},{9,10},{10,1... | collective-permute-start | bytes 4718600 | tf_op jit(solution)/shard_map/while/body/eval_jaxpr/ppermute | solution.py:53
  274.9 51.0 %collective-permute-start.1 = (f32[768,1024]{1,0:T(8,128)}, f32[768,1024]{1,0:T(8,128)}, u32[]{:S(2)}, u32[]{:S(2)}) collective-permute-start(f32[768,1024]{1,0:T(8,128)} %get-tuple-element.206), channel_id=1, source_target_pairs={{0,1},{1,2},{2,3},{3,4},{4,5},{5,6},{6,7},{7,0},{8,9},{9,10},{10,1... | collective-permute-start | bytes 9437192 | tf_op jit(solution)/shard_map/while/body/eval_jaxpr/ppermute | solution.py:54
  310.4 21.7 %copy-start.4 = (f32[768,1024]{1,0:T(8,128)}, f32[768,1024]{1,0:T(8,128)S(1)}, u32[]{:S(2)}) copy-start(f32[768,1024]{1,0:T(8,128)S(1)} %convolution_add_fusion.5) | copy-start | bytes 9437188 | tf_op jit(solution)/shard_map/while
  332.1 19.8 %collective-permute-start = (bf16[768,1024]{1,0:T(8,128)(2,1)}, bf16[768,1024]{1,0:T(8,128)(2,1)}, u32[]{:S(2)}, u32[]{:S(2)}) collective-permute-start(bf16[768,1024]{1,0:T(8,128)(2,1)} %get-tuple-element.205), channel_id=1, source_target_pairs={{0,1},{1,2},{2,3},{3,4},{4,5},{5,6},{6,7},{7,0},{8,9},{9,10},{10,1... | collective-permute-start | bytes 4718600 | tf_op jit(solution)/shard_map/while/body/eval_jaxpr/ppermute | solution.py:53
  334.6 51.0 %collective-permute-start.1 = (f32[768,1024]{1,0:T(8,128)}, f32[768,1024]{1,0:T(8,128)}, u32[]{:S(2)}, u32[]{:S(2)}) collective-permute-start(f32[768,1024]{1,0:T(8,128)} %get-tuple-element.206), channel_id=1, source_target_pairs={{0,1},{1,2},{2,3},{3,4},{4,5},{5,6},{6,7},{7,0},{8,9},{9,10},{10,1... | collective-permute-start | bytes 9437192 | tf_op jit(solution)/shard_map/while/body/eval_jaxpr/ppermute | solution.py:54
  391.9 19.8 %collective-permute-start = (bf16[768,1024]{1,0:T(8,128)(2,1)}, bf16[768,1024]{1,0:T(8,128)(2,1)}, u32[]{:S(2)}, u32[]{:S(2)}) collective-permute-start(bf16[768,1024]{1,0:T(8,128)(2,1)} %get-tuple-element.205), channel_id=1, source_target_pairs={{0,1},{1,2},{2,3},{3,4},{4,5},{5,6},{6,7},{7,0},{8,9},{9,10},{10,1... | collective-permute-start | bytes 4718600 | tf_op jit(solution)/shard_map/while/body/eval_jaxpr/ppermute | solution.py:53
  394.4 51.0 %collective-permute-start.1 = (f32[768,1024]{1,0:T(8,128)}, f32[768,1024]{1,0:T(8,128)}, u32[]{:S(2)}, u32[]{:S(2)}) collective-permute-start(f32[768,1024]{1,0:T(8,128)} %get-tuple-element.206), channel_id=1, source_target_pairs={{0,1},{1,2},{2,3},{3,4},{4,5},{5,6},{6,7},{7,0},{8,9},{9,10},{10,1... | collective-permute-start | bytes 9437192 | tf_op jit(solution)/shard_map/while/body/eval_jaxpr/ppermute | solution.py:54
  451.6 36.7 %collective-permute-start.2 = (f32[768,1024]{1,0:T(8,128)}, f32[768,1024]{1,0:T(8,128)S(1)}, u32[]{:S(2)}, u32[]{:S(2)}) collective-permute-start(f32[768,1024]{1,0:T(8,128)} %get-tuple-element.88), channel_id=1, source_target_pairs={{0,1},{1,2},{2,3},{3,4},{4,5},{5,6},{6,7},{7,0},{8,9},{9,10},{10,1... | collective-permute-start | bytes 9437192 | tf_op jit(solution)/shard_map/ppermute | solution.py:59
  458.8 29.5 %copy-start.1 = (f32[768,1024]{1,0:T(8,128)S(1)}, f32[768,1024]{1,0:T(8,128)}, u32[]{:S(2)}) copy-start(f32[768,1024]{1,0:T(8,128)} %get-tuple-element.125) | copy-start | bytes 9437188
  458.8 29.5 %copy-start.12 = (f32[768]{0:T(1024)S(1)}, f32[768]{0:T(1024)}, u32[]{:S(2)}) copy-start(f32[768]{0:T(1024)} %copy-done.11) | copy-start | bytes 9220
  464.7 24.1 %copy-start.7 = (bf16[768,1024]{1,0:T(8,128)(2,1)S(1)}, bf16[768,1024]{1,0:T(8,128)(2,1)}, u32[]{:S(2)}) copy-start(bf16[768,1024]{1,0:T(8,128)(2,1)} %param.9) | copy-start | bytes 4718596
  (33 other events, 425.0 us)
Sparse Core Ops, SparseCore 0:
  493.2 290.5 all-reduce.2
where the time goes:
time: 804 us; the launch traced here: 802 us
  waiting for transfers between devices  453 us (56%)
  matrix products  165 us (21%)
  blocking collectives  89.4 us (11%)
  local copies, waits for them, and re-layouts  32.6 us (4%)
  starting transfers between devices  20.3 us (3%)
  other arithmetic  18.3 us (2%)
  between operations  18 us (2%)
    psum x1, waiting for transfers between devices, device_body(): lax.psum((dw_img, dw_txt, final_state[3]), ('rep', 'data'))  200 us
    ppermute x7, waiting for transfers between devices, visit_step(): txt_blk = lax.ppermute(txt_blk, 'data', shift_perm)  121 us
    ppermute x7, waiting for transfers between devices, visit_step(): txt_acc = lax.ppermute(txt_acc, 'data', shift_perm)  108 us
    psum x1, blocking collectives, device_body(): lax.psum((dw_img, dw_txt, final_state[3]), ('rep', 'data'))  89.4 us
    dot_general x8, matrix products, tile_terms(): lax.dot_general(img_emb, txt_blk, (((1,), (1,)), ((), ())), preferred_ele...  59.6 us
    dot_general x10, matrix products, contract_rows(): lax.dot_general(left, right, (((0,), (0,)), ((), ())), preferred_element_...  56.6 us
    dot_general x8, matrix products, tile_terms(): img_part = jnp.dot(h_mat, txt_blk, preferred_element_type=jnp.float32)  40.6 us
    ppermute x1, waiting for transfers between devices, device_body(): txt_grad = lax.ppermute(final_state[1], 'data', shift_perm)  23.6 us
  transfers between devices with their start and end apart: 16, of which 16 were waited for; matrix products, arithmetic and copies ran while one was open for 17% of the time, Pallas kernels for 0%

commit v1 on v0

v1 whole, which is shorter than its diff:
```python
import functools

import jax
import jax.numpy as jnp
from jax import lax
from jax.experimental import pallas as pl
from jax.experimental.pallas import tpu as pltpu
from jax.sharding import PartitionSpec as P

F32 = jnp.float32
BF16 = jnp.bfloat16
MESH = pl.DeviceIdType.MESH
X_N, C_N, Y_N, Z_N = 4, 2, 4, 8
VMEM_CAP = 67_043_328


def greet(peers):
    barrier = pltpu.get_barrier_semaphore()
    for peer in peers:
        pl.semaphore_signal(barrier, inc=1, device_id=peer, device_id_type=MESH)
    pl.semaphore_wait(barrier, len(peers))


def remote(src, dst, send_sem, recv_sem, peer):
    return pltpu.make_async_remote_copy(
        src_ref=src, dst_ref=dst, send_sem=send_sem, recv_sem=recv_sem, device_id=peer, device_id_type=MESH
    )


def fold_sum(val):
    rows, cols = val.shape
    return jnp.sum(val.reshape(rows // 8, 8, cols), axis=0)


def fold_log1p(exps):
    rows, cols = exps.shape
    parts = exps.reshape(rows // 8, 8, cols)
    count = rows // 8
    while count > 1:
        if count % 2:
            low, high, tail = parts[: count // 2], parts[count // 2 : count - 1], parts[count - 1 :]
            merged = low + high + low * high
            first = merged[:1]
            first = first + tail + first * tail
            parts = first if count == 3 else jnp.concatenate([first, merged[1:]], axis=0)
        else:
            low, high = parts[: count // 2], parts[count // 2 :]
            parts = low + high + low * high
        count //= 2
    return jnp.log1p(parts[0])


def main_kernel(total_rows, rows, dim, sc_ref, img_ref, txt_ref, wi_ref, wt_ref, dw_ref, scal_ref,
                xq, xk, wq, wk, kbuf, eq, unit, inv, acc, sblk0, sblk1, hblk0, hblk1, sums,
                ld_sem, xs_sem, xr_sem, ks_sem, kr_sem):
    tile = rows // 3
    qt = rows // 2
    rep = lax.axis_index("rep")
    dat = lax.axis_index("data")
    x, c = dat // 2, dat % 2
    kind = x % 2
    step = 1 - 2 * c
    dst_x = (x + step + X_N) % X_N
    src_x = (x - step + X_N) % X_N
    partner = (rep, x * 2 + 1 - c)
    dst = (rep, dst_x * 2 + c)
    src = (rep, src_x * 2 + c)
    scale, bias = sc_ref[0], sc_ref[1]
    h_scale = scale * F32(1.0 / total_rows)
    sblk = (sblk0, sblk1)
    hblk = (hblk0, hblk1)

    def load(from_ref, to_ref, idx):
        return pltpu.make_async_copy(from_ref, to_ref, ld_sem.at[idx])

    own = pl.ds(0, rows)
    swp = pl.ds(rows, rows)

    @pl.when(kind == 0)
    def _():
        load(txt_ref, xk, 0).start()
        load(img_ref, xq.at[own], 1).start()
        load(wi_ref, wq, 2).start()
        load(wt_ref, wk, 3).start()

    @pl.when(kind == 1)
    def _():
        load(img_ref, xk, 0).start()
        load(txt_ref, xq.at[own], 1).start()
        load(wt_ref, wq, 2).start()
        load(wi_ref, wk, 3).start()

    greet((partner, dst, src))
    load(txt_ref, xk, 0).wait()
    swap_copy = remote(xk, xq.at[swp], xs_sem, xr_sem, dst)
    swap_copy.start()

    def krows(slot, t):
        return kbuf.at[slot, pl.ds(pl.multiple_of(t * tile, tile), tile)]

    def erows(base, t):
        return eq.at[pl.ds(pl.multiple_of(base + t * tile, tile), tile)]

    def own_to_dst(t):
        return remote(erows(0, t), krows(4, t), ks_sem.at[0, t], kr_sem.at[4, t], dst)

    def own_to_src(t):
        return remote(erows(0, t), krows(2, t), ks_sem.at[1, t], kr_sem.at[2, t], src)

    def swp_to_dst(t):
        return remote(erows(rows, t), krows(6, t), ks_sem.at[2, t], kr_sem.at[6, t], dst)

    def to_partner(slot, t):
        return remote(krows(slot, t), krows(slot + 1, t), ks_sem.at[3 + slot // 2, t], kr_sem.at[slot + 1, t], partner)

    def got(slot, t):
        remote(krows(slot, t), krows(slot, t), ks_sem.at[0, t], kr_sem.at[slot, t], partner).wait_recv()

    def project_q(base, t):
        at = pl.ds(pl.multiple_of(base + t * tile, tile), tile)
        raw = jnp.dot(xq[at], wq[...], preferred_element_type=F32)
        inv_norm = lax.rsqrt(jnp.sum(raw * raw, axis=1, keepdims=True))
        val = raw * inv_norm
        unit[at] = val
        eq[at] = val.astype(BF16)
        inv[at] = jnp.broadcast_to(inv_norm, (tile, 128))

    def project_k(t):
        at = pl.ds(pl.multiple_of(t * tile, tile), tile)
        raw = jnp.dot(xk[at], wk[...], preferred_element_type=F32)
        inv_norm = lax.rsqrt(jnp.sum(raw * raw, axis=1, keepdims=True))
        kbuf[0, at] = (raw * inv_norm).astype(BF16)

    def send_own(t):
        own_to_src(t).start()
        own_to_dst(t).start()

    load(img_ref, xq.at[own], 1).wait()
    load(wi_ref, wq, 2).wait()

    def own_step(t, carry):
        project_q(0, t)

        @pl.when(t > 0)
        def _():
            send_own(t - 1)

        return carry

    lax.fori_loop(0, 3, own_step, 0)
    load(wt_ref, wk, 3).wait()

    def k_step(t, carry):
        project_k(t)

        @pl.when(t == 0)
        def _():
            send_own(2)

        @pl.when(t > 0)
        def _():
            to_partner(0, t - 1).start()

        return carry

    lax.fori_loop(0, 3, k_step, 0)
    acc[...] = jnp.zeros_like(acc)
    sums[...] = jnp.zeros_like(sums)
    to_partner(0, 2).start()

    def weigh(s_ref, h_ref, j, diag_off):
        dots = s_ref[...]
        margin = dots * scale + bias
        if diag_off is not None:
            row_ids = lax.broadcasted_iota(jnp.int32, dots.shape, 0) + diag_off
            hit = row_ids == lax.broadcasted_iota(jnp.int32, dots.shape, 1)
            margin = jnp.where(hit, -margin, margin)
        exps = jnp.exp(-jnp.abs(margin))
        recip = 1.0 / (1.0 + exps)
        grad = jnp.where(margin >= 0, recip, exps * recip)
        if diag_off is not None:
            grad = jnp.where(hit, -grad, grad)
        h_ref[:, j * tile : (j + 1) * tile] = (grad * h_scale).astype(BF16)
        sums[0] += fold_log1p(exps) + fold_sum(jnp.maximum(margin, 0.0))
        sums[1] += fold_sum(grad * dots)
        sums[2] += fold_sum(grad)

    def attend(q0, tiles, slot, k0, blocks, diag):
        depth = blocks * tile
        cells = [(t, j) for t in range(tiles) for j in range(blocks)]
        pending = []
        half = dim // 2

        def q_at(t):
            return pl.ds(pl.multiple_of(q0 + t * qt, qt), qt)

        def gradient(t, n):
            at = q_at(t)
            cols = slice(n * half, (n + 1) * half)
            keys = kbuf[slot, pl.ds(pl.multiple_of(k0, tile), depth), cols]
            acc[at, cols] += jnp.dot(hblk[t % 2][:, :depth], keys, preferred_element_type=F32)

        for n in range(len(cells) + 1):
            if n < len(cells):
                t, j = cells[n]
                keys = kbuf[slot, pl.ds(pl.multiple_of(k0 + j * tile, tile), tile), :]
                sblk[n % 2][...] = lax.dot_general(eq[q_at(t), :], keys, (((1,), (1,)), ((), ())), preferred_element_type=F32)
            for _ in range(2 if blocks == 1 else 1):
                if pending:
                    gradient(*pending.pop(0))
            if n:
                t, j = cells[n - 1]
                weigh(sblk[(n - 1) % 2], hblk[t % 2], j, t * qt - j * tile if diag else None)
                if j == blocks - 1:
                    pending += [(t, 0), (t, 1)]
        for item in pending:
            gradient(*item)

    def take(slot, forward):
        for t in range(3):
            got(slot, t)
            if forward:
                to_partner(slot, t).start()

    attend(0, 2, 0, 0, 3, True)

    def first_step(i, carry):
        slot = i + 1

        @pl.when(slot == 2)
        def _():
            take(2, True)

        @pl.when(slot != 2)
        def _():
            for t in range(3):
                got(slot, t)

        attend(0, 2, slot, 0, 3, False)
        return carry

    lax.fori_loop(0, 2, first_step, 0)

    swap_copy.wait()

    def swp_step(t, carry):
        project_q(rows, t)

        @pl.when(t > 0)
        def _():
            swp_to_dst(t - 1).start()

        return carry

    lax.fori_loop(0, 3, swp_step, 0)

    def second_step(i, carry):
        @pl.when(i == 0)
        def _():
            swp_to_dst(2).start()

        @pl.when(i == 2)
        def _():
            take(3, False)

        slot = jnp.where(i < 2, i, jnp.where(i == 2, 3, i - 1))
        attend(jnp.where(i == 2, 0, rows), 2, slot, 0, 3, False)
        return carry

    lax.fori_loop(0, 5, second_step, 0)

    take(4, True)
    attend(rows, 2, 4, 0, 3, True)

    def third_step(i, carry):
        @pl.when(i == 1)
        def _():
            take(5, False)

        attend(jnp.where(i == 2, rows, 0), 2, jnp.where(i == 0, 4, 5), 0, 3, False)
        return carry

    lax.fori_loop(0, 3, third_step, 0)

    def last_step(i, carry):
        t, side = i // 2, i % 2

        @pl.when(side == 0)
        def _():
            got(6, t)
            to_partner(6, t).start()

        @pl.when(side == 1)
        def _():
            got(7, t)

        attend(0, 4, 6 + side, t * tile, 1, False)
        return carry

    lax.fori_loop(0, 6, last_step, 0)

    def back_step(t, carry):
        at = pl.ds(pl.multiple_of(t * tile, tile), tile)
        grad, val = acc[at], unit[at]
        proj = jnp.sum(val * grad, axis=1, keepdims=True)
        eq[at] = (inv[at][:, :1] * (grad - val * proj)).astype(BF16)
        return carry

    for t in range(3):
        own_to_dst(t).wait_send()
        own_to_src(t).wait_send()
        swp_to_dst(t).wait_send()
        for slot in (0, 2, 4, 6):
            to_partner(slot, t).wait_send()
    lax.fori_loop(0, 6, back_step, 0)

    def dw_step(t, carry):
        cols = pl.ds(pl.multiple_of(t * 256, 256), 256)
        dw_ref[cols, :] = lax.dot_general(xq[:, cols], eq[...], (((0,), (0,)), ((), ())), preferred_element_type=F32)
        return carry

    lax.fori_loop(0, dim // 256, dw_step, 0)
    lane = jnp.sum(sums[...], axis=1)
    scal_ref[...] = jnp.concatenate([lane[:, :128] + lane[:, 128:], jnp.zeros((5, 128), F32)], axis=0)


def reduce_kernel(n, dw_ref, scal_ref, img_out, txt_out, scal_out,
                  half, ysum, zsum, bufh, bufa, bufb, bufa2, bufb2, part, bufx, mine, other, sc_c, sc_y, sc_z, sc_x,
                  h_sem, a_sem, b_sem, a2_sem, b2_sem, x_sem, c_sem, ga_sem, ha_sem, gb_sem, hb_sem,
                  f_sem, m_sem, o_sem, out_sem):
    cut = (n * 5 // 8) // 128 * 128
    hr = n // 2
    ra, rb = hr // Y_N, hr // Z_N
    rf = hr // (Y_N * Z_N)
    rep = lax.axis_index("rep")
    dat = lax.axis_index("data")
    x, c = dat // 2, dat % 2
    z, y = rep // Y_N, rep % Y_N
    kind = x % 2
    step = 1 - 2 * c
    partner = (rep, x * 2 + 1 - c)
    dst = (rep, (x + step + X_N) % X_N * 2 + c)

    def at_y(d):
        return (z * Y_N + (y + d) % Y_N, dat)

    def at_z(d):
        return ((z + d) % Z_N * Y_N + y, dat)

    def at_x(d):
        return (rep, (x + d) % X_N * 2 + c)

    greet([partner] + [at_y(d) for d in range(1, Y_N)] + [at_z(d) for d in range(1, Z_N)] + [at_x(d) for d in range(1, X_N)])
    col_a, col_b = pl.ds(0, cut), pl.ds(cut, n - cut)

    def rows(start, size):
        return pl.ds(pl.multiple_of(start, 8), size)

    def pair(sem, i, src, dst_ref, peer):
        return remote(src, dst_ref, sem.at[0, i], sem.at[1, i], peer)

    def put(ref, i, peer_list, sem):
        copies = [pair(sem, k, ref.at[i], ref.at[i], peer) for k, peer in enumerate(peer_list)]
        for copy in copies:
            copy.start()
        return copies

    sends = []

    def launch(copy):
        copy.start()
        sends.append(copy)

    sc_c[c] = scal_ref[...]
    h_copy = pair(h_sem, 0, dw_ref.at[rows((1 - c) * hr, hr)], bufh, partner)
    launch(h_copy)
    cc = pair(c_sem, 0, sc_c.at[c], sc_c.at[c], partner)
    launch(cc)
    h_copy.wait_recv()
    half[...] = dw_ref[rows(c * hr, hr), :] + bufh[...]

    a_copies = [pair(a_sem, d - 1, half.at[rows((y + d) % Y_N * ra, ra), col_a], bufa.at[d - 1], at_y(d)) for d in range(1, Y_N)]
    b_copies = [pair(b_sem, d - 1, half.at[rows((z + d) % Z_N * rb, rb), col_b], bufb.at[d - 1], at_z(d)) for d in range(1, Z_N)]
    for copy in a_copies + b_copies:
        launch(copy)
    cc.wait_recv()
    sc_y[y] = sc_c[0] + sc_c[1]
    y_copies = [pair(c_sem, d, sc_y.at[y], sc_y.at[y], at_y(d)) for d in range(1, Y_N)]
    for copy in y_copies:
        launch(copy)

    for copy in a_copies:
        copy.wait_recv()
    tot = half[rows(y * ra, ra), 0:cut]
    for d in range(1, Y_N):
        tot = tot + bufa[d - 1]
    ysum[...] = tot
    a2_copies = [pair(a2_sem, d - 1, ysum.at[rows((z + d) % Z_N * rf, rf)], bufa2.at[d - 1], at_z(d)) for d in range(1, Z_N)]
    for copy in a2_copies:
        launch(copy)
    for copy in b_copies:
        copy.wait_recv()
    tot = half[rows(z * rb, rb), cut:n]
    for d in range(1, Z_N):
        tot = tot + bufb[d - 1]
    zsum[...] = tot
    b2_copies = [pair(b2_sem, d - 1, zsum.at[rows((y + d) % Y_N * rf, rf)], bufb2.at[d - 1], at_y(d)) for d in range(1, Y_N)]
    for copy in b2_copies:
        launch(copy)

    for copy in y_copies:
        copy.wait_recv()
    tot = sc_y[0]
    for i in range(1, Y_N):
        tot = tot + sc_y[i]
    sc_z[z] = tot
    z_copies = [pair(c_sem, Y_N + d, sc_z.at[z], sc_z.at[z], at_z(d)) for d in range(1, Z_N)]
    for copy in z_copies:
        launch(copy)

    for copy in a2_copies:
        copy.wait_recv()
    tot = ysum[rows(z * rf, rf), :]
    for d in range(1, Z_N):
        tot = tot + bufa2[d - 1]
    part[:, 0:cut] = tot
    for copy in b2_copies:
        copy.wait_recv()
    tot = zsum[rows(y * rf, rf), :]
    for d in range(1, Y_N):
        tot = tot + bufb2[d - 1]
    part[:, cut:n] = tot
    x_copy = pair(x_sem, 0, part, bufx, at_x(2))
    launch(x_copy)

    for copy in z_copies:
        copy.wait_recv()
    tot = sc_z[0]
    for i in range(1, Z_N):
        tot = tot + sc_z[i]
    sc_x[x] = tot
    s_copies = [pair(c_sem, Y_N + Z_N + d, sc_x.at[x], sc_x.at[x], at_x(d)) for d in range(1, X_N)]
    for copy in s_copies:
        launch(copy)

    x_copy.wait_recv()
    base = c * hr
    fin_a = rows(base + y * ra + z * rf, rf)
    fin_b = rows(base + z * rb + y * rf, rf)
    mine[fin_a, 0:cut] = part[:, 0:cut] + bufx[:, 0:cut]
    mine[fin_b, cut:n] = part[:, cut:n] + bufx[:, cut:n]

    def same(sem, i, ref, at, peer):
        return pair(sem, i, ref.at[at], ref.at[at], peer)

    ga = [same(ga_sem, d - 1, mine, (fin_a, col_a), at_z(d)) for d in range(1, Z_N)]
    gb = [same(gb_sem, d - 1, mine, (fin_b, col_b), at_y(d)) for d in range(1, Y_N)]
    for copy in gb + ga:
        launch(copy)
    for copy in s_copies:
        copy.wait_recv()
    tot = sc_x[0]
    for i in range(1, X_N):
        tot = tot + sc_x[i]
    scal_out[...] = tot

    def piece(i):
        if i < Y_N:
            return (rows(base + (y - i + Y_N) % Y_N * ra, ra), col_a)
        i -= Y_N
        return (rows(base + (z - i + Z_N) % Z_N * rb, rb), col_b)

    def partner_piece(i):
        pbase = (1 - c) * hr
        if i < Y_N:
            return (rows(pbase + (y - i + Y_N) % Y_N * ra, ra), col_a)
        i -= Y_N
        return (rows(pbase + (z - i + Z_N) % Z_N * rb, rb), col_b)

    def spread(i):
        launch(pair(f_sem, i, mine.at[piece(i)], other.at[piece(i)], dst))
        launch(same(m_sem, i, mine, piece(i), partner))

    for copy in gb:
        copy.wait_recv()
    hb = [same(hb_sem, d - 1, mine, piece(Y_N), at_z(d)) for d in range(1, Z_N)]
    for copy in hb:
        launch(copy)
    spread(Y_N)
    for copy in ga:
        copy.wait_recv()
    ha = [same(ha_sem, d - 1, mine, piece(0), at_y(d)) for d in range(1, Y_N)]
    for copy in ha:
        launch(copy)
    spread(0)

    def wait_piece(copy_sem, i, at):
        pair(copy_sem, i, mine.at[at], mine.at[at], partner).wait_recv()

    ring = [(min(d, Z_N - d) / Z_N, hb_sem, d) for d in range(1, Z_N)] + [(min(d, Y_N - d) / Y_N, ha_sem, d) for d in range(1, Y_N)]
    order = [(sem, d) for _, sem, d in sorted(ring, key=lambda item: item[0])]
    arrived = [Y_N, 0]
    for sem, d in order:
        i = d if sem is ha_sem else Y_N + d
        wait_piece(sem, d - 1, piece(i))
        spread(i)
        arrived.append(i)
    for i in arrived:
        pair(f_sem, i, other.at[piece(i)], other.at[piece(i)], dst).wait_recv()
        launch(same(o_sem, i, other, piece(i), partner))
    for i in arrived:
        wait_piece(m_sem, i, partner_piece(i))
    for i in arrived:
        wait_piece(o_sem, i, partner_piece(i))
    for copy in sends:
        copy.wait_send()

    def store(i, from_ref, to_ref):
        return pltpu.make_async_copy(from_ref, to_ref, out_sem.at[i])

    @pl.when(kind == 0)
    def _():
        store(0, mine, img_out).start()
        store(1, other, txt_out).start()

    @pl.when(kind == 1)
    def _():
        store(0, mine, txt_out).start()
        store(1, other, img_out).start()

    store(0, mine, img_out).wait()
    store(1, other, txt_out).wait()


def pair_sems(count):
    return pltpu.SemaphoreType.DMA((2, count))


def head_gradients(img_loc, txt_loc, w_img, w_txt, log_temp, logit_bias, total_rows):
    rows, dim = img_loc.shape
    temp_scale = jnp.exp(log_temp)
    sc = jnp.stack([temp_scale, logit_bias])
    any_spec = pl.BlockSpec(memory_space=pl.ANY)
    vmem_spec = pl.BlockSpec(memory_space=pltpu.VMEM)
    tile, qt = rows // 3, rows // 2
    dma = pltpu.SemaphoreType.DMA
    flops = 2 * rows * dim * dim * 7 + 4 * 2 * rows * 8 * rows * dim
    dw, scal = pl.pallas_call(
        functools.partial(main_kernel, total_rows, rows, dim),
        out_shape=(jax.ShapeDtypeStruct((dim, dim), F32), jax.ShapeDtypeStruct((8, 128), F32)),
        in_specs=[pl.BlockSpec(memory_space=pltpu.SMEM)] + [any_spec] * 4,
        out_specs=(vmem_spec, vmem_spec),
        scratch_shapes=[
            pltpu.VMEM((2 * rows, dim), BF16),
            pltpu.VMEM((rows, dim), BF16),
            pltpu.VMEM((dim, dim), BF16),
            pltpu.VMEM((dim, dim), BF16),
            pltpu.VMEM((8, rows, dim), BF16),
            pltpu.VMEM((2 * rows, dim), BF16),
            pltpu.VMEM((2 * rows, dim), F32),
            pltpu.VMEM((2 * rows, 128), F32),
            pltpu.VMEM((2 * rows, dim), F32),
            pltpu.VMEM((qt, tile), F32),
            pltpu.VMEM((qt, tile), F32),
            pltpu.VMEM((qt, rows), BF16),
            pltpu.VMEM((qt, rows), BF16),
            pltpu.VMEM((3, 8, tile), F32),
            dma((4,)), dma, dma, dma((7, 3)), dma((8, 3)),
        ],
        compiler_params=pltpu.CompilerParams(collective_id=0, has_side_effects=True, vmem_limit_bytes=VMEM_CAP),
        cost_estimate=pl.CostEstimate(flops=flops, bytes_accessed=16 << 20, transcendentals=0),
        name="contrast",
    )(sc, img_loc, txt_loc, w_img, w_txt)

    cut = (dim * 5 // 8) // 128 * 128
    hr = dim // 2
    ra, rb, rf = hr // Y_N, hr // Z_N, hr // (Y_N * Z_N)
    nb = dim - cut
    dw_img, dw_txt, scal = pl.pallas_call(
        functools.partial(reduce_kernel, dim),
        out_shape=(jax.ShapeDtypeStruct((dim, dim), F32), jax.ShapeDtypeStruct((dim, dim), F32), jax.ShapeDtypeStruct((8, 128), F32)),
        in_specs=[vmem_spec, vmem_spec],
        out_specs=(any_spec, any_spec, vmem_spec),
        scratch_shapes=[
            pltpu.VMEM((hr, dim), F32),
            pltpu.VMEM((ra, cut), F32),
            pltpu.VMEM((rb, nb), F32),
            pltpu.VMEM((hr, dim), F32),
            pltpu.VMEM((Y_N - 1, ra, cut), F32),
            pltpu.VMEM((Z_N - 1, rb, nb), F32),
            pltpu.VMEM((Z_N - 1, rf, cut), F32),
            pltpu.VMEM((Y_N - 1, rf, nb), F32),
            pltpu.VMEM((rf, dim), F32),
            pltpu.VMEM((rf, dim), F32),
            pltpu.VMEM((dim, dim), F32),
            pltpu.VMEM((dim, dim), F32),
            pltpu.VMEM((C_N, 8, 128), F32),
            pltpu.VMEM((Y_N, 8, 128), F32),
            pltpu.VMEM((Z_N, 8, 128), F32),
            pltpu.VMEM((X_N, 8, 128), F32),
            pair_sems(1), pair_sems(Y_N - 1), pair_sems(Z_N - 1), pair_sems(Z_N - 1), pair_sems(Y_N - 1),
            pair_sems(1), pair_sems(X_N + Y_N + Z_N), pair_sems(Z_N - 1), pair_sems(Y_N - 1), pair_sems(Y_N - 1),
            pair_sems(Z_N - 1), pair_sems(Y_N + Z_N), pair_sems(Y_N + Z_N), pair_sems(Y_N + Z_N), dma((2,)),
        ],
        compiler_params=pltpu.CompilerParams(collective_id=1, has_side_effects=True, vmem_limit_bytes=VMEM_CAP),
        name="head_sum",
    )(dw, scal)
    tot = jnp.sum(scal, axis=1) * 0.5
    inv_n = F32(1.0 / total_rows)
    return tot[0] * inv_n, temp_scale * tot[1] * inv_n, tot[2] * inv_n, dw_img, dw_txt


def solution(mesh):
    devices = mesh.shape["rep"] * mesh.shape["data"]
    row_spec = P(("rep", "data"), None)

    def device_body(img_loc, txt_loc, w_img, w_txt, log_temp, logit_bias):
        return head_gradients(img_loc, txt_loc, w_img, w_txt, log_temp, logit_bias, img_loc.shape[0] * devices)

    return jax.shard_map(device_body, mesh=mesh, in_specs=(row_spec, row_spec, P(), P(), P(), P()), out_specs=(P(), P(), P(), P(), P()), check_vma=False)
```

time: 804 us -> 219 us (0.27)
  waiting for transfers between devices: 453 us -> 0 us
  Pallas kernels: 0 us -> 202 us
  matrix products: 165 us -> 0 us
  blocking collectives: 89.4 us -> 0 us
  local copies, waits for them, and re-layouts: 32.6 us -> 7.55 us
  starting transfers between devices: 20.3 us -> 0 us
  other arithmetic: 18.3 us -> 1.38 us
  between operations: 18 us -> 7.33 us
    ppermute x15 -> x0, waiting for transfers between devices: 253 us -> none  [the longest x7 121 us: visit_step(): txt_blk = lax.ppermute(txt_blk, 'data', shift_perm)]
    pallas_call x0 -> x2, Pallas kernels: none -> 202 us  [the longest x1 104 us: head_gradients(): pl.pallas_call(functools.partial(main_kernel, total_rows, rows, dim), out...]
    psum x1 -> x0, waiting for transfers between devices: 200 us -> none  [device_body(): lax.psum((dw_img, dw_txt, final_state[3]), ('rep', 'data'))]
    dot_general x28 -> x0, matrix products: 165 us -> none  [the longest x8 59.6 us: tile_terms(): lax.dot_general(img_emb, txt_blk, (((1,), (1,)), ((), ())), preferred_ele...]
    psum x1 -> x0, blocking collectives: 89.4 us -> none  [device_body(): lax.psum((dw_img, dw_txt, final_state[3]), ('rep', 'data'))]
    ppermute x15 -> x0, starting transfers between devices: 20.3 us -> none  [the longest x7 17.6 us: visit_step(): txt_blk = lax.ppermute(txt_blk, 'data', shift_perm)]
    while x63 -> x0, local copies, waits for them, and re-layouts: 20 us -> none
    add x14 -> x0, other arithmetic: 9.79 us -> none  [the longest x7 9.77 us: visit_step(): scal_acc + scal_part]
  transfers between devices with their start and end apart: 16 -> 0, of which waited for: 16 -> 0; matrix products, arithmetic and copies ran while one was open for 17% -> 0% of each run, Pallas kernels for 0% -> 0%
where the time goes in v1:
time: 219 us; the launch traced here: 218 us
  Pallas kernels  202 us (92%)
  local copies, waits for them, and re-layouts  7.55 us (3%)
  between operations  7.33 us (3%)
    pallas_call x1, Pallas kernels, head_gradients(): pl.pallas_call(functools.partial(main_kernel, total_rows, rows, dim), out...  104 us
    pallas_call x1, Pallas kernels, head_gradients(): pl.pallas_call(functools.partial(reduce_kernel, dim), out_shape=(jax.Shap...  97.7 us
    unnamed x4, local copies, waits for them, and re-layouts  6.96 us

profile of v1, /device:TPU:1, one launch (start us, length us, event | category | flops | bytes accessed | tf_op | source)
XLA Modules:
  0.0 218.4 jit_solution(3062244578941610019)
XLA Ops:
  2.0 0.6 pad_maximum_fusion.sc_ref
  2.5 104.4 %contrast.1 = (f32[1024,1024]{1,0:T(8,128)}, f32[8,128]{1,0:T(8,128)}) custom-call(f32[2]{0:T(128)} %pad_maximum_fusion.sc_ref, bf16[768,1024]{1,0:T(8,128)(2,1)} %img_ref.1, bf16[768,1024]{1,0:T(8,128)(2,1)} %txt_ref.1, bf16[1024,1024]{1,0:T(8,128)(2,1)} %wi_ref.1, bf16[1024,1024]{1,0:T(8,128)(2,1)} %wt_ref.1), custom_call_target="tpu_custom_call" | custom-call | flops 49928994816 | bytes 16777216 | tf_op jit(solution)/shard_map/contrast/pallas_call | solution.py:548
  107.0 97.7 %head_sum.1 = (f32[1024,1024]{1,0:T(8,128)}, f32[1024,1024]{1,0:T(8,128)}, f32[8,128]{1,0:T(8,128)}) custom-call(f32[1024,1024]{1,0:T(8,128)} %get-tuple-element.10.dw_ref, f32[8,128]{1,0:T(8,128)} %get-tuple-element.11.scal_ref), custom_call_target="tpu_custom_call" | custom-call | tf_op jit(solution)/shard_map/head_sum/pallas_call | solution.py:579
  204.7 0.8 reduce_sum.9
  205.5 0.6 fusion
  208.0 0.0 copy-start
  208.0 4.9 %copy.15 = f32[1024,1024]{1,0:T(8,128)} copy(f32[1024,1024]{1,0:T(8,128)} %get-tuple-element.26) | data formatting | bytes 8388608
  213.0 0.0 copy-done
  213.0 2.0 copy.16
  (1 shorter events, 0.0 us)
Async XLA Ops:
  208.0 5.0 %copy-start = (f32[1024,1024]{1,0:T(8,128)S(1)}, f32[1024,1024]{1,0:T(8,128)}, u32[]{:S(2)}) copy-start(f32[1024,1024]{1,0:T(8,128)} %get-tuple-element.27) | copy-start | bytes 12582916

commit v2 on v0

v2 whole, which is shorter than its diff:
```python
import functools

import jax
import jax.numpy as jnp
from jax import lax
from jax.experimental import pallas as pl
from jax.experimental.pallas import tpu as pltpu
from jax.sharding import PartitionSpec as P

F32 = jnp.float32
BF16 = jnp.bfloat16
MESH = pl.DeviceIdType.MESH
X_N, C_N, Y_N, Z_N = 4, 2, 4, 8
VMEM_CAP = 55 << 20


def greet(peers):
    barrier = pltpu.get_barrier_semaphore()
    for peer in peers:
        pl.semaphore_signal(barrier, inc=1, device_id=peer, device_id_type=MESH)
    pl.semaphore_wait(barrier, len(peers))


def remote(src, dst, send_sem, recv_sem, peer):
    return pltpu.make_async_remote_copy(
        src_ref=src, dst_ref=dst, send_sem=send_sem, recv_sem=recv_sem, device_id=peer, device_id_type=MESH
    )


def fold_sum(val):
    rows, cols = val.shape
    return jnp.sum(val.reshape(rows // 8, 8, cols), axis=0)


def whole_kernel(total_rows, rows, dim, cut, sc_ref, img_ref, txt_ref, wi_ref, wt_ref, img_out, txt_out, scal_out,
                xq, xk, wq, wk, kbuf, eq, unit, inv, acc, sblk0, sblk1, hblk0, hblk1, sums, away, landed,
                half,
                ysum, zsum, ylow, yhigh, yring, bufb, bufa2, bufb2, part, bufx, sc_c, sc_y, sc_z, sc_x,
                ld_sem, xs_sem, xr_sem, es_sem, er_sem, ps_sem, pr_sem, hs_sem, hr_sem,
                l_sem, k_sem, b_sem, a2_sem, b2_sem, x_sem, c_sem, ga_sem, ha_sem, gb_sem, hb_sem,
                f_sem, m_sem, o_sem, fin_sem):
    n = dim
    tile = rows // 3
    qt = rows // 2
    rep = lax.axis_index("rep")
    dat = lax.axis_index("data")
    x, c = dat // 2, dat % 2
    kind = x % 2
    step = 1 - 2 * c
    dst_x = (x + step + X_N) % X_N
    src_x = (x - step + X_N) % X_N
    partner = (rep, x * 2 + 1 - c)
    dst = (rep, dst_x * 2 + c)
    src = (rep, src_x * 2 + c)
    scale, bias = sc_ref[0], sc_ref[1]
    h_scale = scale * F32(1.0 / total_rows)
    log2_e = F32(1.4426950408889634)
    scale2, bias2 = scale * log2_e, bias * log2_e
    sblk = (sblk0, sblk1)
    hblk = (hblk0, hblk1)

    z, y = rep // Y_N, rep % Y_N

    def at_y(d):
        return (z * Y_N + (y + d + Y_N) % Y_N, dat)

    def at_z(d):
        return ((z + d) % Z_N * Y_N + y, dat)

    def at_x(d):
        return (rep, (x + d) % X_N * 2 + c)

    up, down = at_y(1), at_y(-1)

    def load(from_ref, to_ref, idx):
        return pltpu.make_async_copy(from_ref, to_ref, ld_sem.at[idx])

    own = pl.ds(0, rows)
    swp = pl.ds(rows, rows)

    @pl.when(kind == 0)
    def _():
        load(txt_ref, xk, 0).start()
        load(img_ref, xq.at[own], 1).start()
        load(wi_ref, wq, 2).start()
        load(wt_ref, wk, 3).start()

    @pl.when(kind == 1)
    def _():
        load(img_ref, xk, 0).start()
        load(txt_ref, xq.at[own], 1).start()
        load(wt_ref, wq, 2).start()
        load(wi_ref, wk, 3).start()

    greet([partner] + [at_y(d) for d in range(1, Y_N)] + [at_z(d) for d in range(1, Z_N)] + [at_x(d) for d in range(1, X_N)])
    load(txt_ref, xk, 0).wait()
    swap_copy = remote(xk, xq.at[swp], xs_sem, xr_sem, dst)
    swap_copy.start()

    def direct(g):
        return kbuf.at[g, pl.ds(0, tile)]

    def passed(g):
        return kbuf.at[g, pl.ds(tile, tile)]

    def erows(base, t):
        return eq.at[pl.ds(pl.multiple_of(base + t * tile, tile), tile)]

    def own_to_src(t):
        return remote(erows(0, t), direct(3 + t), es_sem.at[t], er_sem.at[t], src)

    def own_to_dst(t):
        return remote(erows(0, t), direct(6 + t), es_sem.at[3 + t], er_sem.at[3 + t], dst)

    def swp_to_dst(t):
        return remote(erows(rows, t), direct(9 + t), es_sem.at[6 + t], er_sem.at[6 + t], dst)

    def got_direct(g):
        remote(direct(g), direct(g), es_sem.at[0], er_sem.at[g - 3], partner).wait_recv()

    def pass_own(t):
        return remote(direct(t), passed(t), ps_sem.at[t], pr_sem.at[t], partner)

    def pass_on(g):
        return remote(direct(g), passed(g + 1), ps_sem.at[g], pr_sem.at[g], partner)

    def got_passed(i):
        remote(passed(0), passed(0), ps_sem.at[i], pr_sem.at[i], partner).wait_recv()

    def project_q(base, t):
        at = pl.ds(pl.multiple_of(base + t * tile, tile), tile)
        raw = jnp.dot(xq[at], wq[...], preferred_element_type=F32)
        inv_norm = lax.rsqrt(jnp.sum(raw * raw, axis=1, keepdims=True))
        val = raw * inv_norm
        unit[at] = val
        eq[at] = val.astype(BF16)
        inv[at] = jnp.broadcast_to(inv_norm, (tile, 128))

    def project_k(t):
        at = pl.ds(pl.multiple_of(t * tile, tile), tile)
        raw = jnp.dot(xk[at], wk[...], preferred_element_type=F32)
        inv_norm = lax.rsqrt(jnp.sum(raw * raw, axis=1, keepdims=True))
        kbuf[t, :tile] = (raw * inv_norm).astype(BF16)

    load(wt_ref, wk, 3).wait()

    def k_step(t, carry):
        project_k(t)

        @pl.when(t > 0)
        def _():
            pass_own(t - 1).start()

        return carry

    lax.fori_loop(0, 3, k_step, 0)
    load(img_ref, xq.at[own], 1).wait()
    load(wi_ref, wq, 2).wait()

    def own_step(t, carry):
        project_q(0, t)

        @pl.when(t == 0)
        def _():
            pass_own(2).start()

        return carry

    lax.fori_loop(0, 3, own_step, 0)
    acc[...] = jnp.zeros_like(acc)
    sums[...] = jnp.zeros_like(sums)

    def weigh(s_ref, h_ref, j, diag_off):
        loss, temp, tilt, lift = None, None, None, None
        for r in range(0, qt, 32):
            dots = s_ref[r : r + 32, slice(j * tile, (j + 1) * tile)]
            logit = dots * scale2 + bias2
            if diag_off is not None:
                row_ids = lax.broadcasted_iota(jnp.int32, dots.shape, 0) + (diag_off + r)
                hit = row_ids == lax.broadcasted_iota(jnp.int32, dots.shape, 1)
                logit = jnp.where(hit, -logit, logit)
            exps = jnp.exp2(jnp.minimum(logit, -logit))
            grad = jnp.exp2(jnp.minimum(logit, 0.0)) * (1.0 / (1.0 + exps))
            if diag_off is not None:
                grad = jnp.where(hit, -grad, grad)
            h_ref[r : r + 32, j * tile : (j + 1) * tile] = (grad * h_scale).astype(BF16)
            parts = [exps[i : i + 8] for i in range(0, 32, 8)]
            while len(parts) > 1:
                parts = [a + b + a * b for a, b in zip(parts[::2], parts[1::2])]
            one, two, three = fold_sum(grad * dots), fold_sum(grad), fold_sum(jnp.maximum(logit, 0.0))
            if r:
                loss = loss + parts[0] + loss * parts[0]
                temp, tilt, lift = temp + one, tilt + two, lift + three
            else:
                loss, temp, tilt, lift = parts[0], one, two, three
        sums[0] += jnp.log1p(loss)
        sums[1] += temp
        sums[2] += tilt
        sums[3] += lift

    def attend(q0, tiles, g, k0, blocks, diag_from, key_tile):
        depth = blocks * tile
        pending = []
        mid = dim // 2

        def gradient(t, n):
            at = slice(q0 + t * qt, q0 + (t + 1) * qt)
            cols = slice(n * mid, (n + 1) * mid)
            acc[at, cols] += jnp.dot(hblk[t % 2][:, :depth], kbuf[g, k0 : k0 + depth, cols], preferred_element_type=F32)

        for t in range(tiles + 1):
            if t < tiles:
                ques = eq[q0 + t * qt : q0 + (t + 1) * qt, :]
                sblk[t % 2][:, :depth] = lax.dot_general(ques, kbuf[g, k0 : k0 + depth, :], (((1,), (1,)), ((), ())), preferred_element_type=F32)
            for item in pending:
                gradient(*item)
            pending = []
            if t:
                for j in range(blocks):
                    diag = diag_from is not None and t - 1 >= diag_from and j == 0
                    weigh(sblk[(t - 1) % 2], hblk[(t - 1) % 2], j, (t - 1 - diag_from) * qt - key_tile * tile if diag else None)
                pending = [(t - 1, 0), (t - 1, 1)]
        for item in pending:
            gradient(*item)

    def first_step(t, carry):
        got_passed(t)
        attend(0, 2, t, 0, 2, 0, t)
        return carry

    lax.fori_loop(0, 3, first_step, 0)

    swap_copy.wait_send()
    for t in range(3):
        own_to_src(t).start()
    swap_copy.wait_recv()

    def swp_step(t, carry):
        project_q(rows, t)
        return carry

    lax.fori_loop(0, 3, swp_step, 0)

    def second_step(t, carry):
        @pl.when(t == 2)
        def _():
            for i in range(3):
                own_to_dst(i).start()
            for i in range(3):
                swp_to_dst(i).start()
            got_direct(3)
            pass_on(3).start()

        attend(rows, 2, t, 0, 2, None, None)
        return carry

    lax.fori_loop(0, 3, second_step, 0)
    attend(0, 4, 3, 0, 1, None, None)

    def main_step(g, carry):
        got_direct(g)
        pass_on(g).start()
        got_passed(g - 1)
        twin = (g >= 6) & (g < 9)

        @pl.when(twin)
        def _():
            attend(0, 4, g, 0, 2, 2, g - 6)

        @pl.when(jnp.logical_not(twin))
        def _():
            attend(0, 4, g, 0, 2, None, None)

        return carry

    lax.fori_loop(4, 12, main_step, 0)
    got_passed(11)
    attend(0, 4, 12, tile, 1, None, None)

    for t in range(3):
        own_to_src(t).wait_send()
        own_to_dst(t).wait_send()
        swp_to_dst(t).wait_send()

    def back_step(t, carry):
        at = pl.ds(pl.multiple_of(t * tile, tile), tile)
        grad, val = acc[at], unit[at]
        proj = jnp.sum(val * grad, axis=1, keepdims=True)
        eq[at] = (inv[at][:, :1] * (grad - val * proj)).astype(BF16)
        return carry

    lax.fori_loop(0, 6, back_step, 0)

    strip = dim // 8
    hrows = dim // 2

    def head(row0, n):
        cols = pl.ds(pl.multiple_of(row0, strip), n)
        return lax.dot_general(xq[:, cols], eq[...], (((0,), (0,)), ((), ())), preferred_element_type=F32)

    def give(t):
        at = pl.ds(pl.multiple_of(t * 2 * strip, strip), 2 * strip)
        return remote(away.at[at], landed.at[at], hs_sem.at[t], hr_sem.at[t], partner)

    def away_step(t, carry):
        away[pl.ds(pl.multiple_of(t * 2 * strip, strip), 2 * strip), :] = head((1 - c) * hrows + t * 2 * strip, 2 * strip)

        @pl.when(t == 1)
        def _():
            give(0).start()

        return carry

    lax.fori_loop(0, 2, away_step, 0)
    give(1).start()

    def home_step(t, carry):
        at = pl.ds(pl.multiple_of(t * 2 * strip, strip), 2 * strip)
        half[at, :] = head(c * hrows + t * 2 * strip, 2 * strip)
        return carry

    lax.fori_loop(0, 2, home_step, 0)
    give(0).wait_recv()
    give(1).wait_recv()

    def join_step(t, carry):
        at = pl.ds(pl.multiple_of(t * strip, strip), strip)
        half[at, :] += landed[at, :]
        return carry

    lax.fori_loop(0, 4, join_step, 0)
    lane = jnp.sum(sums[...], axis=1)
    lane = lane[:, :128] + lane[:, 128:]
    loss = lane[:1] + lane[3:] * F32(0.6931471805599453)
    sc_c[c] = jnp.concatenate([loss, lane[1:3], jnp.zeros((5, 128), F32)], axis=0)
    for t in range(2):
        give(t).wait_send()
    for t in range(3):
        pass_own(t).wait_send()
    for g in range(3, 12):
        pass_on(g).wait_send()

    hr = n // 2
    ra, rb = hr // Y_N, hr // Z_N
    rf = hr // (Y_N * Z_N)
    hh = ra // 2
    col_a, col_b = pl.ds(0, cut), pl.ds(cut, n - cut)

    def rows(start, size):
        return pl.ds(pl.multiple_of(start, 8), size)

    def pair(sem, i, src, dst_ref, peer):
        return remote(src, dst_ref, sem.at[0, i], sem.at[1, i], peer)

    sends = []

    def launch(copy):
        copy.start()
        sends.append(copy)

    def block_y(d, part_rows=None):
        first, size = part_rows or (0, ra)
        return rows((y + d + Y_N) % Y_N * ra + first, size)

    low, high = (0, hh), (hh, hh)

    low_in = pair(l_sem, 0, half.at[block_y(2, low), col_a], ylow, up)
    high_in = pair(l_sem, 1, half.at[block_y(2, high), col_a], yhigh, down)
    own_up = pair(k_sem, 0, half.at[block_y(1, high), col_a], yring.at[0, pl.ds(hh, hh)], up)
    own_down = pair(k_sem, 1, half.at[block_y(-1, low), col_a], yring.at[1, pl.ds(0, hh)], down)
    sum_up = pair(k_sem, 2, ylow, yring.at[0, pl.ds(0, hh)], up)
    sum_down = pair(k_sem, 3, yhigh, yring.at[1, pl.ds(hh, hh)], down)
    b_copies = [pair(b_sem, d - 1, half.at[rows((z + d) % Z_N * rb, rb), col_b], bufb.at[d - 1], at_z(d)) for d in range(1, Z_N)]
    for copy in [low_in, high_in, own_up, own_down] + b_copies:
        launch(copy)
    cc = pair(c_sem, 0, sc_c.at[c], sc_c.at[c], partner)
    launch(cc)
    low_in.wait_recv()
    ylow[...] += half[block_y(1, low), 0:cut]
    high_in.wait_recv()
    yhigh[...] += half[block_y(-1, high), 0:cut]
    launch(sum_up)
    launch(sum_down)
    cc.wait_recv()
    sc_y[y] = sc_c[0] + sc_c[1]
    y_copies = [pair(c_sem, d, sc_y.at[y], sc_y.at[y], at_y(d)) for d in range(1, Y_N)]
    for copy in y_copies:
        launch(copy)

    for copy in [own_up, own_down, sum_up, sum_down]:
        copy.wait_recv()
    ysum[...] = (half[block_y(0), 0:cut] + yring[0]) + yring[1]
    a2_copies = [pair(a2_sem, d - 1, ysum.at[rows((z + d) % Z_N * rf, rf)], bufa2.at[d - 1], at_z(d)) for d in range(1, Z_N)]
    for copy in a2_copies:
        launch(copy)
    for copy in b_copies:
        copy.wait_recv()
    tot = half[rows(z * rb, rb), cut:n]
    for d in range(1, Z_N):
        tot = tot + bufb[d - 1]
    zsum[...] = tot
    b2_copies = [pair(b2_sem, d - 1, zsum.at[rows((y + d) % Y_N * rf, rf)], bufb2.at[d - 1], at_y(d)) for d in range(1, Y_N)]
    for copy in b2_copies:
        launch(copy)

    for copy in y_copies:
        copy.wait_recv()
    tot = sc_y[0]
    for i in range(1, Y_N):
        tot = tot + sc_y[i]
    sc_z[z] = tot
    z_copies = [pair(c_sem, Y_N + d, sc_z.at[z], sc_z.at[z], at_z(d)) for d in range(1, Z_N)]
    for copy in z_copies:
        launch(copy)

    for copy in a2_copies:
        copy.wait_recv()
    tot = ysum[rows(z * rf, rf), :]
    for d in range(1, Z_N):
        tot = tot + bufa2[d - 1]
    part[:, 0:cut] = tot
    for copy in b2_copies:
        copy.wait_recv()
    tot = zsum[rows(y * rf, rf), :]
    for d in range(1, Y_N):
        tot = tot + bufb2[d - 1]
    part[:, cut:n] = tot
    x_copy = pair(x_sem, 0, part, bufx.at[0], at_x(2))
    launch(x_copy)

    for copy in z_copies:
        copy.wait_recv()
    tot = sc_z[0]
    for i in range(1, Z_N):
        tot = tot + sc_z[i]
    sc_x[x] = tot
    s_copies = [pair(c_sem, Y_N + Z_N + d, sc_x.at[x], sc_x.at[x], at_x(d)) for d in range(1, X_N)]
    for copy in s_copies:
        launch(copy)

    x_copy.wait_recv()
    bufx[1] = part[...] + bufx[0]
    base = c * hr
    fin_a = rows(base + y * ra + z * rf, rf)
    fin_b = rows(base + z * rb + y * rf, rf)

    def by_kind(act):
        @pl.when(kind == 0)
        def _():
            act(img_out, txt_out)

        @pl.when(kind == 1)
        def _():
            act(txt_out, img_out)

    def same(sem, i, ref, at, peer):
        return pair(sem, i, ref.at[at], ref.at[at], peer)

    def put(mine, i, col, at):
        return pltpu.make_async_copy(bufx.at[1, :, col], mine.at[at, col], fin_sem.at[i])

    def gather_b(mine, d):
        return pair(gb_sem, d - 1, bufx.at[1, :, col_b], mine.at[fin_b, col_b], at_y(d))

    def gather_a(mine, d):
        return pair(ga_sem, d - 1, bufx.at[1, :, col_a], mine.at[fin_a, col_a], at_z(d))

    def first_gather(mine, other):
        for d in range(1, Y_N):
            gather_b(mine, d).start()
        for d in range(1, Z_N):
            gather_a(mine, d).start()
        put(mine, 0, col_a, fin_a).start()
        put(mine, 1, col_b, fin_b).start()

    by_kind(first_gather)
    for copy in s_copies:
        copy.wait_recv()
    tot = sc_x[0]
    for i in range(1, X_N):
        tot = tot + sc_x[i]
    scal_out[...] = tot
    put(img_out, 0, col_a, fin_a).wait()
    put(img_out, 1, col_b, fin_b).wait()

    def piece(i, core):
        if i < Y_N:
            return (rows(core * hr + (y - i + Y_N) % Y_N * ra, ra), col_a)
        return (rows(core * hr + (z - i + Y_N + Z_N) % Z_N * rb, rb), col_b)

    def quarter(d, part_rows):
        return (rows(base + (y + d + Y_N) % Y_N * ra + part_rows[0], part_rows[1]), col_a)

    def forward(mine, i):
        return pair(f_sem, i, mine.at[piece(i, c)], mine.at[piece(i, c)], dst)

    def spread(mine, other, i):
        forward(mine, i).start()
        same(m_sem, i, mine, piece(i, c), partner).start()

    def over_z(mine, d):
        return same(hb_sem, d - 1, mine, piece(Y_N, c), at_z(d))

    def full(mine, i):
        return same(ha_sem, i, mine, piece(0, c), up if i == 0 else down)

    def onward(mine, i):
        return same(ha_sem, 2 + i, mine, quarter(-1, low) if i == 0 else quarter(1, high), up if i == 0 else down)

    for d in range(1, Y_N):
        gather_b(img_out, d).wait_recv()

    def second_b(mine, other):
        for d in range(1, Z_N):
            over_z(mine, d).start()
        spread(mine, other, Y_N)

    by_kind(second_b)
    for d in range(1, Z_N):
        gather_a(img_out, d).wait_recv()

    def second_a(mine, other):
        full(mine, 0).start()
        full(mine, 1).start()
        spread(mine, other, 0)

    by_kind(second_a)

    def z_piece(d):
        same(hb_sem, d - 1, img_out, piece(Y_N + d, c), partner).wait_recv()

    z_piece(1)
    z_piece(Z_N - 1)
    for i in range(2):
        full(img_out, i).wait_recv()

    def third(mine, other):
        onward(mine, 0).start()
        onward(mine, 1).start()
        for i in (Y_N + 1, Y_N + Z_N - 1, 1, 3):
            spread(mine, other, i)

    by_kind(third)
    arrived = [Y_N, 0, Y_N + 1, Y_N + Z_N - 1, 1, 3]
    near = [d // 2 + 1 if d % 2 == 0 else Z_N - d // 2 - 1 for d in range(2, Z_N - 1)]
    for d in near[:2]:
        z_piece(d)
    by_kind(lambda mine, other: [spread(mine, other, Y_N + d) for d in near[:2]] and None)
    onward(img_out, 0).wait_recv()
    onward(img_out, 1).wait_recv()
    by_kind(lambda mine, other: spread(mine, other, 2))
    for d in near[2:]:
        z_piece(d)
    by_kind(lambda mine, other: [spread(mine, other, Y_N + d) for d in near[2:]] and None)
    arrived += [Y_N + d for d in near[:2]] + [2] + [Y_N + d for d in near[2:]]

    def across(group):
        for i in group:
            forward(img_out, i).wait_recv()
        by_kind(lambda mine, other: [same(o_sem, i, other, piece(i, c), partner).start() for i in group] and None)

    for at in range(0, len(arrived), 3):
        across(arrived[at : at + 3])
    for i in arrived:
        same(m_sem, i, img_out, piece(i, 1 - c), partner).wait_recv()
    for i in arrived:
        same(o_sem, i, img_out, piece(i, 1 - c), partner).wait_recv()
    for copy in sends:
        copy.wait_send()
    for d in range(1, Y_N):
        gather_b(img_out, d).wait_send()
    for d in range(1, Z_N):
        gather_a(img_out, d).wait_send()
        over_z(img_out, d).wait_send()
    for i in range(2):
        full(img_out, i).wait_send()
        onward(img_out, i).wait_send()
    for i in arrived:
        forward(img_out, i).wait_send()
        same(m_sem, i, img_out, piece(i, c), partner).wait_send()
        same(o_sem, i, img_out, piece(i, c), partner).wait_send()


def pair_sems(count):
    return pltpu.SemaphoreType.DMA((2, count))


def head_gradients(img_loc, txt_loc, w_img, w_txt, log_temp, logit_bias, total_rows):
    rows, dim = img_loc.shape
    temp_scale = jnp.exp(log_temp)
    sc = jnp.stack([temp_scale, logit_bias])
    any_spec = pl.BlockSpec(memory_space=pl.ANY)
    vmem_spec = pl.BlockSpec(memory_space=pltpu.VMEM)
    tile, qt = rows // 3, rows // 2
    dma = pltpu.SemaphoreType.DMA
    flops = 2 * rows * dim * dim * 7 + 4 * 2 * rows * 8 * rows * dim
    cut = (dim * 3 // 4) // 128 * 128
    hr = dim // 2
    ra, rb, rf = hr // Y_N, hr // Z_N, hr // (Y_N * Z_N)
    nb = dim - cut
    head = jax.ShapeDtypeStruct((dim, dim), F32)
    vmem = pltpu.VMEM
    dw_img, dw_txt, scal = pl.pallas_call(
        functools.partial(whole_kernel, total_rows, rows, dim, cut),
        out_shape=(head, head, jax.ShapeDtypeStruct((8, 128), F32)),
        in_specs=[pl.BlockSpec(memory_space=pltpu.SMEM)] + [any_spec] * 4,
        out_specs=(any_spec, any_spec, vmem_spec),
        scratch_shapes=[
            vmem((2 * rows, dim), BF16),
            vmem((rows, dim), BF16),
            vmem((dim, dim), BF16),
            vmem((dim, dim), BF16),
            vmem((13, 2 * tile, dim), BF16),
            vmem((2 * rows, dim), BF16),
            vmem((2 * rows, dim), F32),
            vmem((2 * rows, 128), F32),
            vmem((2 * rows, dim), F32),
            vmem((qt, 2 * tile), F32),
            vmem((qt, 2 * tile), F32),
            vmem((qt, 2 * tile), BF16),
            vmem((qt, 2 * tile), BF16),
            vmem((4, 8, tile), F32),
            vmem((hr, dim), F32),
            vmem((hr, dim), F32),
            vmem((hr, dim), F32),
            vmem((ra, cut), F32),
            vmem((rb, nb), F32),
            vmem((ra // 2, cut), F32),
            vmem((ra // 2, cut), F32),
            vmem((2, ra, cut), F32),
            vmem((Z_N - 1, rb, nb), F32),
            vmem((Z_N - 1, rf, cut), F32),
            vmem((Y_N - 1, rf, nb), F32),
            vmem((rf, dim), F32),
            vmem((2, rf, dim), F32),
            vmem((C_N, 8, 128), F32),
            vmem((Y_N, 8, 128), F32),
            vmem((Z_N, 8, 128), F32),
            vmem((X_N, 8, 128), F32),
            dma((4,)), dma, dma, dma((9,)), dma((9,)), dma((12,)), dma((12,)), dma((2,)), dma((2,)),
            pair_sems(2), pair_sems(4), pair_sems(Z_N - 1), pair_sems(Z_N - 1), pair_sems(Y_N - 1),
            pair_sems(1), pair_sems(X_N + Y_N + Z_N), pair_sems(Z_N - 1), pair_sems(4), pair_sems(Y_N - 1),
            pair_sems(Z_N - 1), pair_sems(Y_N + Z_N), pair_sems(Y_N + Z_N), pair_sems(Y_N + Z_N), dma((2,)),
        ],
        compiler_params=pltpu.CompilerParams(collective_id=0, has_side_effects=True, vmem_limit_bytes=VMEM_CAP),
        cost_estimate=pl.CostEstimate(flops=flops, bytes_accessed=16 << 20, transcendentals=0),
        name="contrast",
    )(sc, img_loc, txt_loc, w_img, w_txt)
    tot = jnp.sum(scal, axis=1) * 0.5
    inv_n = F32(1.0 / total_rows)
    return tot[0] * inv_n, temp_scale * tot[1] * inv_n, tot[2] * inv_n, dw_img, dw_txt


def solution(mesh):
    devices = mesh.shape["rep"] * mesh.shape["data"]
    row_spec = P(("rep", "data"), None)

    def device_body(img_loc, txt_loc, w_img, w_txt, log_temp, logit_bias):
        return head_gradients(img_loc, txt_loc, w_img, w_txt, log_temp, logit_bias, img_loc.shape[0] * devices)

    return jax.shard_map(device_body, mesh=mesh, in_specs=(row_spec, row_spec, P(), P(), P(), P()), out_specs=(P(), P(), P(), P(), P()), check_vma=False)
```

time: 804 us -> 198 us (0.25)
  waiting for transfers between devices: 453 us -> 0 us
  Pallas kernels: 0 us -> 182 us
  matrix products: 165 us -> 0 us
  blocking collectives: 89.4 us -> 0 us
  local copies, waits for them, and re-layouts: 32.6 us -> 7.55 us
  starting transfers between devices: 20.3 us -> 0 us
  other arithmetic: 18.3 us -> 1.39 us
  between operations: 18 us -> 7.32 us
    ppermute x15 -> x0, waiting for transfers between devices: 253 us -> none  [the longest x7 121 us: visit_step(): txt_blk = lax.ppermute(txt_blk, 'data', shift_perm)]
    psum x1 -> x0, waiting for transfers between devices: 200 us -> none  [device_body(): lax.psum((dw_img, dw_txt, final_state[3]), ('rep', 'data'))]
    pallas_call x0 -> x1, Pallas kernels: none -> 182 us  [head_gradients(): pl.pallas_call(functools.partial(whole_kernel, total_rows, rows, dim, cut...]
    dot_general x28 -> x0, matrix products: 165 us -> none  [the longest x8 59.6 us: tile_terms(): lax.dot_general(img_emb, txt_blk, (((1,), (1,)), ((), ())), preferred_ele...]
    psum x1 -> x0, blocking collectives: 89.4 us -> none  [device_body(): lax.psum((dw_img, dw_txt, final_state[3]), ('rep', 'data'))]
    ppermute x15 -> x0, starting transfers between devices: 20.3 us -> none  [the longest x7 17.6 us: visit_step(): txt_blk = lax.ppermute(txt_blk, 'data', shift_perm)]
    while x63 -> x0, local copies, waits for them, and re-layouts: 20 us -> none
    add x14 -> x0, other arithmetic: 9.79 us -> none  [the longest x7 9.77 us: visit_step(): scal_acc + scal_part]
  transfers between devices with their start and end apart: 16 -> 0, of which waited for: 16 -> 0; matrix products, arithmetic and copies ran while one was open for 17% -> 0% of each run, Pallas kernels for 0% -> 0%
where the time goes in v2:
time: 198 us
  Pallas kernels  182 us (92%)
  local copies, waits for them, and re-layouts  7.55 us (4%)
  between operations  7.32 us (4%)
    pallas_call x1, Pallas kernels, head_gradients(): pl.pallas_call(functools.partial(whole_kernel, total_rows, rows, dim, cut...  182 us
    unnamed x4, local copies, waits for them, and re-layouts  6.96 us

profile of v2, /device:TPU:1, one launch (start us, length us, event | category | flops | bytes accessed | tf_op | source)
XLA Modules:
  0.0 197.8 jit_solution(17349239154142140282)
XLA Ops:
  2.0 0.6 pad_maximum_fusion.sc_ref
  2.5 181.5 %contrast.1 = (f32[1024,1024]{1,0:T(8,128)}, f32[1024,1024]{1,0:T(8,128)}, f32[8,128]{1,0:T(8,128)}) custom-call(f32[2]{0:T(128)} %pad_maximum_fusion.sc_ref, bf16[768,1024]{1,0:T(8,128)(2,1)} %img_ref.1, bf16[768,1024]{1,0:T(8,128)(2,1)} %txt_ref.1, bf16[1024,1024]{1,0:T(8,128)(2,1)} %wi_ref.1, bf16[1024,1024]{1,0:T(8,128)(2,1)} %wt_ref.1), custom_call_target="tpu_custom_call" | custom-call | flops 49928994816 | bytes 16777216 | tf_op jit(solution)/shard_map/contrast/pallas_call | solution.py:603
  184.1 0.8 reduce_sum.9
  184.9 0.6 fusion
  187.5 0.0 copy-start
  187.5 4.9 %copy.15 = f32[1024,1024]{1,0:T(8,128)} copy(f32[1024,1024]{1,0:T(8,128)} %get-tuple-element.22) | data formatting | bytes 8388608
  192.4 0.0 copy-done
  192.4 2.0 %copy.16 = f32[1024,1024]{1,0:T(8,128)} copy(f32[1024,1024]{1,0:T(8,128)S(1)} %copy-done) | data formatting | bytes 8388608
  (1 shorter events, 0.0 us)
Async XLA Ops:
  187.5 5.0 %copy-start = (f32[1024,1024]{1,0:T(8,128)S(1)}, f32[1024,1024]{1,0:T(8,128)}, u32[]{:S(2)}) copy-start(f32[1024,1024]{1,0:T(8,128)} %get-tuple-element.23) | copy-start | bytes 12582916

commit v3 on v2

--- a/solution.py
+++ b/solution.py
@@ -11,7 +11,7 @@
 BF16 = jnp.bfloat16
 MESH = pl.DeviceIdType.MESH
 X_N, C_N, Y_N, Z_N = 4, 2, 4, 8
-VMEM_CAP = 55 << 20
+VMEM_CAP = 67_043_328
 
 
 def greet(peers):
@@ -32,7 +32,8 @@
     return jnp.sum(val.reshape(rows // 8, 8, cols), axis=0)
 
 
-def whole_kernel(total_rows, rows, dim, cut, sc_ref, img_ref, txt_ref, wi_ref, wt_ref, img_out, txt_out, scal_out,
+def whole_kernel(total_rows, rows, dim, cut, lt_ref, lb_ref, img_ref, txt_ref, wi_ref, wt_ref,
+                 img_out, txt_out, loss_out, temp_out, bias_out,
                 xq, xk, wq, wk, kbuf, eq, unit, inv, acc, sblk0, sblk1, hblk0, hblk1, sums, away, landed,
                 half,
                 ysum, zsum, ylow, yhigh, yring, bufb, bufa2, bufb2, part, bufx, sc_c, sc_y, sc_z, sc_x,
@@ -52,10 +53,10 @@
     partner = (rep, x * 2 + 1 - c)
     dst = (rep, dst_x * 2 + c)
     src = (rep, src_x * 2 + c)
-    scale, bias = sc_ref[0], sc_ref[1]
-    h_scale = scale * F32(1.0 / total_rows)
+    inv_n = F32(1.0 / total_rows)
     log2_e = F32(1.4426950408889634)
-    scale2, bias2 = scale * log2_e, bias * log2_e
+    temp = jnp.exp(jnp.full((1, tile), lt_ref[0], F32))
+    h_scale, scale2, bias2 = temp * inv_n, temp * log2_e, lb_ref[0] * log2_e
     sblk = (sblk0, sblk1)
     hblk = (hblk0, hblk1)
 
@@ -364,41 +365,50 @@
 
     low, high = (0, hh), (hh, hh)
 
-    low_in = pair(l_sem, 0, half.at[block_y(2, low), col_a], ylow, up)
-    high_in = pair(l_sem, 1, half.at[block_y(2, high), col_a], yhigh, down)
-    own_up = pair(k_sem, 0, half.at[block_y(1, high), col_a], yring.at[0, pl.ds(hh, hh)], up)
-    own_down = pair(k_sem, 1, half.at[block_y(-1, low), col_a], yring.at[1, pl.ds(0, hh)], down)
-    sum_up = pair(k_sem, 2, ylow, yring.at[0, pl.ds(0, hh)], up)
-    sum_down = pair(k_sem, 3, yhigh, yring.at[1, pl.ds(hh, hh)], down)
+    wide = cut // 2
+    cols = [pl.ds(h * wide, wide) for h in range(2)]
+    span = [slice(h * wide, (h + 1) * wide) for h in range(2)]
+    low_in = [pair(l_sem, h, half.at[block_y(2, low), cols[h]], ylow.at[:, cols[h]], up) for h in range(2)]
+    high_in = [pair(l_sem, 2 + h, half.at[block_y(2, high), cols[h]], yhigh.at[:, cols[h]], down) for h in range(2)]
+    own_up = [pair(k_sem, h, half.at[block_y(1, high), cols[h]], yring.at[0, pl.ds(hh, hh), cols[h]], up) for h in range(2)]
+    own_down = [pair(k_sem, 2 + h, half.at[block_y(-1, low), cols[h]], yring.at[1, pl.ds(0, hh), cols[h]], down) for h in range(2)]
+    sum_up = [pair(k_sem, 4 + h, ylow.at[:, cols[h]], yring.at[0, pl.ds(0, hh), cols[h]], up) for h in range(2)]
+    sum_down = [pair(k_sem, 6 + h, yhigh.at[:, cols[h]], yring.at[1, pl.ds(hh, hh), cols[h]], down) for h in range(2)]
     b_copies = [pair(b_sem, d - 1, half.at[rows((z + d) % Z_N * rb, rb), col_b], bufb.at[d - 1], at_z(d)) for d in range(1, Z_N)]
-    for copy in [low_in, high_in, own_up, own_down] + b_copies:
+    for copy in low_in + high_in + b_copies + own_up + own_down:
         launch(copy)
     cc = pair(c_sem, 0, sc_c.at[c], sc_c.at[c], partner)
     launch(cc)
-    low_in.wait_recv()
-    ylow[...] += half[block_y(1, low), 0:cut]
-    high_in.wait_recv()
-    yhigh[...] += half[block_y(-1, high), 0:cut]
-    launch(sum_up)
-    launch(sum_down)
+    for h in range(2):
+        low_in[h].wait_recv()
+        ylow[:, span[h]] += half[block_y(1, low), span[h]]
+        high_in[h].wait_recv()
+        launch(sum_up[h])
+        yhigh[:, span[h]] += half[block_y(-1, high), span[h]]
+        launch(sum_down[h])
     cc.wait_recv()
     sc_y[y] = sc_c[0] + sc_c[1]
     y_copies = [pair(c_sem, d, sc_y.at[y], sc_y.at[y], at_y(d)) for d in range(1, Y_N)]
     for copy in y_copies:
         launch(copy)
 
-    for copy in [own_up, own_down, sum_up, sum_down]:
-        copy.wait_recv()
-    ysum[...] = (half[block_y(0), 0:cut] + yring[0]) + yring[1]
-    a2_copies = [pair(a2_sem, d - 1, ysum.at[rows((z + d) % Z_N * rf, rf)], bufa2.at[d - 1], at_z(d)) for d in range(1, Z_N)]
-    for copy in a2_copies:
-        launch(copy)
+    def straight(h, d):
+        i = h * (Z_N - 1) + d - 1
+        return pair(a2_sem, i, ysum.at[rows((z + d) % Z_N * rf, rf), cols[h]], bufa2.at[d - 1, :, cols[h]], at_z(d))
+
     for copy in b_copies:
         copy.wait_recv()
     tot = half[rows(z * rb, rb), cut:n]
     for d in range(1, Z_N):
         tot = tot + bufb[d - 1]
     zsum[...] = tot
+    a2_copies = [[straight(h, d) for d in range(1, Z_N)] for h in range(2)]
+    for h in range(2):
+        for copies in (own_up, own_down, sum_up, sum_down):
+            copies[h].wait_recv()
+        ysum[:, span[h]] = (half[block_y(0), span[h]] + yring[0, :, span[h]]) + yring[1, :, span[h]]
+        for copy in a2_copies[h]:
+            launch(copy)
     b2_copies = [pair(b2_sem, d - 1, zsum.at[rows((y + d) % Y_N * rf, rf)], bufb2.at[d - 1], at_y(d)) for d in range(1, Y_N)]
     for copy in b2_copies:
         launch(copy)
@@ -413,20 +423,23 @@
     for copy in z_copies:
         launch(copy)
 
-    for copy in a2_copies:
-        copy.wait_recv()
-    tot = ysum[rows(z * rf, rf), :]
-    for d in range(1, Z_N):
-        tot = tot + bufa2[d - 1]
-    part[:, 0:cut] = tot
-    for copy in b2_copies:
-        copy.wait_recv()
-    tot = zsum[rows(y * rf, rf), :]
-    for d in range(1, Y_N):
-        tot = tot + bufb2[d - 1]
-    part[:, cut:n] = tot
-    x_copy = pair(x_sem, 0, part, bufx.at[0], at_x(2))
-    launch(x_copy)
+    x_cols = [cols[0], pl.ds(wide, n - wide)]
+    x_copies = [pair(x_sem, h, part.at[:, x_cols[h]], bufx.at[0, :, x_cols[h]], at_x(2)) for h in range(2)]
+    for h in range(2):
+        for copy in a2_copies[h]:
+            copy.wait_recv()
+        tot = ysum[rows(z * rf, rf), span[h]]
+        for d in range(1, Z_N):
+            tot = tot + bufa2[d - 1, :, span[h]]
+        part[:, span[h]] = tot
+        if h:
+            for copy in b2_copies:
+                copy.wait_recv()
+            tot = zsum[rows(y * rf, rf), :]
+            for d in range(1, Y_N):
+                tot = tot + bufb2[d - 1]
+            part[:, cut:n] = tot
+        launch(x_copies[h])
 
     for copy in z_copies:
         copy.wait_recv()
@@ -438,8 +451,6 @@
     for copy in s_copies:
         launch(copy)
 
-    x_copy.wait_recv()
-    bufx[1] = part[...] + bufx[0]
     base = c * hr
     fin_a = rows(base + y * ra + z * rf, rf)
     fin_b = rows(base + z * rb + y * rf, rf)
@@ -456,40 +467,54 @@
     def same(sem, i, ref, at, peer):
         return pair(sem, i, ref.at[at], ref.at[at], peer)
 
-    def put(mine, i, col, at):
+    def put(mine, i):
+        at, col = (fin_b, col_b) if i == 2 else (fin_a, cols[i])
         return pltpu.make_async_copy(bufx.at[1, :, col], mine.at[at, col], fin_sem.at[i])
 
     def gather_b(mine, d):
         return pair(gb_sem, d - 1, bufx.at[1, :, col_b], mine.at[fin_b, col_b], at_y(d))
 
-    def gather_a(mine, d):
-        return pair(ga_sem, d - 1, bufx.at[1, :, col_a], mine.at[fin_a, col_a], at_z(d))
-
-    def first_gather(mine, other):
+    def gather_a(mine, h, d):
+        return pair(ga_sem, h * (Z_N - 1) + d - 1, bufx.at[1, :, cols[h]], mine.at[fin_a, cols[h]], at_z(d))
+
+    def start_a(mine, other, h):
+        for d in range(1, Z_N):
+            gather_a(mine, h, d).start()
+        put(mine, h).start()
+
+    def start_b(mine, other):
         for d in range(1, Y_N):
             gather_b(mine, d).start()
-        for d in range(1, Z_N):
-            gather_a(mine, d).start()
-        put(mine, 0, col_a, fin_a).start()
-        put(mine, 1, col_b, fin_b).start()
-
-    by_kind(first_gather)
+        put(mine, 2).start()
+
+    x_copies[0].wait_recv()
+    bufx[1, :, span[0]] = part[:, span[0]] + bufx[0, :, span[0]]
+    by_kind(lambda mine, other: start_a(mine, other, 0))
+    x_copies[1].wait_recv()
+    bufx[1, :, wide:n] = part[:, wide:n] + bufx[0, :, wide:n]
+    by_kind(start_b)
+    by_kind(lambda mine, other: start_a(mine, other, 1))
     for copy in s_copies:
         copy.wait_recv()
     tot = sc_x[0]
     for i in range(1, X_N):
         tot = tot + sc_x[i]
-    scal_out[...] = tot
-    put(img_out, 0, col_a, fin_a).wait()
-    put(img_out, 1, col_b, fin_b).wait()
+    tot = tot * (F32(0.5) * inv_n)
+    loss_out[0, 0] = jnp.sum(tot[0:1])
+    temp_out[0, 0] = jnp.sum(tot[1:2] * temp[:, :128])
+    bias_out[0, 0] = jnp.sum(tot[2:3])
+    for i in range(3):
+        put(img_out, i).wait()
+
+    first_z = 2 * Y_N
 
     def piece(i, core):
-        if i < Y_N:
-            return (rows(core * hr + (y - i + Y_N) % Y_N * ra, ra), col_a)
-        return (rows(core * hr + (z - i + Y_N + Z_N) % Z_N * rb, rb), col_b)
-
-    def quarter(d, part_rows):
-        return (rows(base + (y + d + Y_N) % Y_N * ra + part_rows[0], part_rows[1]), col_a)
+        if i < first_z:
+            return (rows(core * hr + (y - i // 2 + Y_N) % Y_N * ra, ra), cols[i % 2])
+        return (rows(core * hr + (z - i + first_z + Z_N) % Z_N * rb, rb), col_b)
+
+    def quarter(d, part_rows, h):
+        return (rows(base + (y + d + Y_N) % Y_N * ra + part_rows[0], part_rows[1]), cols[h])
 
     def forward(mine, i):
         return pair(f_sem, i, mine.at[piece(i, c)], mine.at[piece(i, c)], dst)
@@ -499,68 +524,90 @@
         same(m_sem, i, mine, piece(i, c), partner).start()
 
     def over_z(mine, d):
-        return same(hb_sem, d - 1, mine, piece(Y_N, c), at_z(d))
-
-    def full(mine, i):
-        return same(ha_sem, i, mine, piece(0, c), up if i == 0 else down)
-
-    def onward(mine, i):
-        return same(ha_sem, 2 + i, mine, quarter(-1, low) if i == 0 else quarter(1, high), up if i == 0 else down)
-
-    for d in range(1, Y_N):
-        gather_b(img_out, d).wait_recv()
+        return same(hb_sem, d - 1, mine, piece(first_z, c), at_z(d))
+
+    def full(mine, i, h):
+        return same(ha_sem, 2 * h + i, mine, piece(h, c), up if i == 0 else down)
+
+    def onward(mine, i, h):
+        return same(ha_sem, 4 + 2 * h + i, mine, quarter(-1, low, h) if i == 0 else quarter(1, high, h), up if i == 0 else down)
+
+    arrived = []
+
+    def second_a(h):
+        for d in range(1, Z_N):
+            gather_a(img_out, h, d).wait_recv()
+
+        def act(mine, other):
+            full(mine, 0, h).start()
+            full(mine, 1, h).start()
+            spread(mine, other, h)
+
+        by_kind(act)
+        arrived.append(h)
 
     def second_b(mine, other):
         for d in range(1, Z_N):
             over_z(mine, d).start()
-        spread(mine, other, Y_N)
-
+        spread(mine, other, first_z)
+
+    def z_pieces(ds):
+        for d in ds:
+            same(hb_sem, d - 1, img_out, piece(first_z + d, c), partner).wait_recv()
+            arrived.append(first_z + d)
+
+        def act(mine, other):
+            for d in ds:
+                spread(mine, other, first_z + d)
+
+        by_kind(act)
+
+    def third_a(h):
+        for i in range(2):
+            full(img_out, i, h).wait_recv()
+
+        def act(mine, other):
+            onward(mine, 0, h).start()
+            onward(mine, 1, h).start()
+            spread(mine, other, 2 + h)
+            spread(mine, other, 6 + h)
+
+        by_kind(act)
+        arrived.extend([2 + h, 6 + h])
+
+    def fourth_a(h):
+        for i in range(2):
+            onward(img_out, i, h).wait_recv()
+        by_kind(lambda mine, other: spread(mine, other, 4 + h))
+        arrived.append(4 + h)
+
+    second_a(0)
+    for d in range(1, Y_N):
+        gather_b(img_out, d).wait_recv()
     by_kind(second_b)
-    for d in range(1, Z_N):
-        gather_a(img_out, d).wait_recv()
-
-    def second_a(mine, other):
-        full(mine, 0).start()
-        full(mine, 1).start()
-        spread(mine, other, 0)
-
-    by_kind(second_a)
-
-    def z_piece(d):
-        same(hb_sem, d - 1, img_out, piece(Y_N + d, c), partner).wait_recv()
-
-    z_piece(1)
-    z_piece(Z_N - 1)
-    for i in range(2):
-        full(img_out, i).wait_recv()
-
-    def third(mine, other):
-        onward(mine, 0).start()
-        onward(mine, 1).start()
-        for i in (Y_N + 1, Y_N + Z_N - 1, 1, 3):
-            spread(mine, other, i)
-
-    by_kind(third)
-    arrived = [Y_N, 0, Y_N + 1, Y_N + Z_N - 1, 1, 3]
-    near = [d // 2 + 1 if d % 2 == 0 else Z_N - d // 2 - 1 for d in range(2, Z_N - 1)]
-    for d in near[:2]:
-        z_piece(d)
-    by_kind(lambda mine, other: [spread(mine, other, Y_N + d) for d in near[:2]] and None)
-    onward(img_out, 0).wait_recv()
-    onward(img_out, 1).wait_recv()
-    by_kind(lambda mine, other: spread(mine, other, 2))
-    for d in near[2:]:
-        z_piece(d)
-    by_kind(lambda mine, other: [spread(mine, other, Y_N + d) for d in near[2:]] and None)
-    arrived += [Y_N + d for d in near[:2]] + [2] + [Y_N + d for d in near[2:]]
+    arrived.append(first_z)
+    second_a(1)
+    third_a(0)
+    z_pieces([1, Z_N - 1])
+    third_a(1)
+    z_pieces([2, Z_N - 2])
+    fourth_a(0)
+    z_pieces([3, Z_N - 3])
+    fourth_a(1)
+    z_pieces(list(range(4, Z_N - 3)))
 
     def across(group):
         for i in group:
             forward(img_out, i).wait_recv()
-        by_kind(lambda mine, other: [same(o_sem, i, other, piece(i, c), partner).start() for i in group] and None)
-
-    for at in range(0, len(arrived), 3):
-        across(arrived[at : at + 3])
+
+        def act(mine, other):
+            for i in group:
+                same(o_sem, i, other, piece(i, c), partner).start()
+
+        by_kind(act)
+
+    for at in range(0, len(arrived), 2):
+        across(arrived[at : at + 2])
     for i in arrived:
         same(m_sem, i, img_out, piece(i, 1 - c), partner).wait_recv()
     for i in arrived:
@@ -570,27 +617,48 @@
     for d in range(1, Y_N):
         gather_b(img_out, d).wait_send()
     for d in range(1, Z_N):
-        gather_a(img_out, d).wait_send()
         over_z(img_out, d).wait_send()
-    for i in range(2):
-        full(img_out, i).wait_send()
-        onward(img_out, i).wait_send()
+        for h in range(2):
+            gather_a(img_out, h, d).wait_send()
+    for h in range(2):
+        for i in range(2):
+            full(img_out, i, h).wait_send()
+            onward(img_out, i, h).wait_send()
     for i in arrived:
         forward(img_out, i).wait_send()
         same(m_sem, i, img_out, piece(i, c), partner).wait_send()
         same(o_sem, i, img_out, piece(i, c), partner).wait_send()
 
 
+def place_kernel(img_in, txt_in, img_out, txt_out, stage, in_sem, out_sem):
+    parts, size, _ = stage.shape
+
+    def copies(i):
+        from_ref, to_ref = (img_in, img_out) if i < parts // 2 else (txt_in, txt_out)
+        at = pl.ds(i % (parts // 2) * size, size)
+        return (
+            pltpu.make_async_copy(from_ref.at[at], stage.at[i], in_sem.at[i]),
+            pltpu.make_async_copy(stage.at[i], to_ref.at[at], out_sem.at[i]),
+        )
+
+    for i in range(parts):
+        copies(i)[0].start()
+    for i in range(parts):
+        come, go = copies(i)
+        come.wait()
+        go.start()
+    for i in range(parts):
+        copies(i)[1].wait()
+
+
 def pair_sems(count):
     return pltpu.SemaphoreType.DMA((2, count))
 
 
 def head_gradients(img_loc, txt_loc, w_img, w_txt, log_temp, logit_bias, total_rows):
     rows, dim = img_loc.shape
-    temp_scale = jnp.exp(log_temp)
-    sc = jnp.stack([temp_scale, logit_bias])
     any_spec = pl.BlockSpec(memory_space=pl.ANY)
-    vmem_spec = pl.BlockSpec(memory_space=pltpu.VMEM)
+    smem_spec = pl.BlockSpec(memory_space=pltpu.SMEM)
     tile, qt = rows // 3, rows // 2
     dma = pltpu.SemaphoreType.DMA
     flops = 2 * rows * dim * dim * 7 + 4 * 2 * rows * 8 * rows * dim
@@ -600,11 +668,11 @@
     nb = dim - cut
     head = jax.ShapeDtypeStruct((dim, dim), F32)
     vmem = pltpu.VMEM
-    dw_img, dw_txt, scal = pl.pallas_call(
+    dw_img, dw_txt, loss, d_temp, d_bias = pl.pallas_call(
         functools.partial(whole_kernel, total_rows, rows, dim, cut),
-        out_shape=(head, head, jax.ShapeDtypeStruct((8, 128), F32)),
-        in_specs=[pl.BlockSpec(memory_space=pltpu.SMEM)] + [any_spec] * 4,
-        out_specs=(any_spec, any_spec, vmem_spec),
+        out_shape=(head, head) + (jax.ShapeDtypeStruct((1, 1), F32),) * 3,
+        in_specs=[smem_spec] * 2 + [any_spec] * 4,
+        out_specs=(any_spec, any_spec, smem_spec, smem_spec, smem_spec),
         scratch_shapes=[
             vmem((2 * rows, dim), BF16),
             vmem((rows, dim), BF16),
@@ -638,17 +706,24 @@
             vmem((Z_N, 8, 128), F32),
             vmem((X_N, 8, 128), F32),
             dma((4,)), dma, dma, dma((9,)), dma((9,)), dma((12,)), dma((12,)), dma((2,)), dma((2,)),
-            pair_sems(2), pair_sems(4), pair_sems(Z_N - 1), pair_sems(Z_N - 1), pair_sems(Y_N - 1),
-            pair_sems(1), pair_sems(X_N + Y_N + Z_N), pair_sems(Z_N - 1), pair_sems(4), pair_sems(Y_N - 1),
-            pair_sems(Z_N - 1), pair_sems(Y_N + Z_N), pair_sems(Y_N + Z_N), pair_sems(Y_N + Z_N), dma((2,)),
+            pair_sems(4), pair_sems(8), pair_sems(Z_N - 1), pair_sems(2 * (Z_N - 1)), pair_sems(Y_N - 1),
+            pair_sems(2), pair_sems(X_N + Y_N + Z_N), pair_sems(2 * (Z_N - 1)), pair_sems(8), pair_sems(Y_N - 1),
+            pair_sems(Z_N - 1), pair_sems(2 * Y_N + Z_N), pair_sems(2 * Y_N + Z_N), pair_sems(2 * Y_N + Z_N), dma((3,)),
         ],
         compiler_params=pltpu.CompilerParams(collective_id=0, has_side_effects=True, vmem_limit_bytes=VMEM_CAP),
         cost_estimate=pl.CostEstimate(flops=flops, bytes_accessed=16 << 20, transcendentals=0),
         name="contrast",
-    )(sc, img_loc, txt_loc, w_img, w_txt)
-    tot = jnp.sum(scal, axis=1) * 0.5
-    inv_n = F32(1.0 / total_rows)
-    return tot[0] * inv_n, temp_scale * tot[1] * inv_n, tot[2] * inv_n, dw_img, dw_txt
+    )(log_temp.reshape(1), logit_bias.reshape(1), img_loc, txt_loc, w_img, w_txt)
+    dw_img, dw_txt = pl.pallas_call(
+        place_kernel,
+        out_shape=(head, head),
+        in_specs=[any_spec, any_spec],
+        out_specs=(any_spec, any_spec),
+        scratch_shapes=[vmem((8, dim // 4, dim), F32), dma((8,)), dma((8,))],
+        compiler_params=pltpu.CompilerParams(vmem_limit_bytes=VMEM_CAP),
+        name="place",
+    )(dw_img, dw_txt)
+    return loss.reshape(()), d_temp.reshape(()), d_bias.reshape(()), dw_img, dw_txt
 
 
 def solution(mesh):

time: 198 us -> 184 us (0.929)
  local copies, waits for them, and re-layouts: 7.55 us -> 0 us
  Pallas kernels: 182 us -> 177 us
    pallas_call x1, Pallas kernels: 182 us -> 171 us  [head_gradients(): pl.pallas_call(functools.partial(whole_kernel, total_rows, rows, dim, cut...]
    unnamed x4 -> x0, local copies, waits for them, and re-layouts: 6.96 us -> none
    pallas_call x0 -> x1, Pallas kernels: none -> 6.42 us  [head_gradients(): pl.pallas_call(place_kernel, out_shape=(head, head), in_specs=[any_spec,...]
where the time goes in v3:
time: 184 us
  Pallas kernels  177 us (96%)
  between operations  7.06 us (4%)
    pallas_call x1, Pallas kernels, head_gradients(): pl.pallas_call(functools.partial(whole_kernel, total_rows, rows, dim, cut...  171 us
    pallas_call x1, Pallas kernels, head_gradients(): pl.pallas_call(place_kernel, out_shape=(head, head), in_specs=[any_spec,...  6.42 us

profile of v3, /device:TPU:1, one launch (start us, length us, event | category | flops | bytes accessed | tf_op | source)
XLA Modules:
  0.0 184.2 jit_solution(4127252532187906185)
XLA Ops:
  1.9 170.7 %contrast.1 = (f32[1024,1024]{1,0:T(8,128)}, f32[1024,1024]{1,0:T(8,128)}, f32[1,1]{1,0:T(1,128)}, f32[1,1]{1,0:T(1,128)}, f32[1,1]{1,0:T(1,128)}) custom-call(f32[1]{0:T(128)} %bitcast.5.lt_ref, f32[1]{0:T(128)} %bitcast.6.lb_ref, bf16[768,1024]{1,0:T(8,128)(2,1)} %img_ref.1, bf16[768,1024]{1,0:T(8,128)(2,1)} %txt_ref.1, bf16[1024,1024]{1,0:T(8,128)(2,1)} %wi_ref.1, ...), custom_call_target="tpu_custom_call" | custom-call | flops 49928994816 | bytes 16777216 | tf_op jit(solution)/shard_map/contrast/pallas_call | solution.py:671
  172.6 6.4 %place.1 = (f32[1024,1024]{1,0:T(8,128)}, f32[1024,1024]{1,0:T(8,128)}) custom-call(f32[1024,1024]{1,0:T(8,128)} %get-tuple-element.15.img_in, f32[1024,1024]{1,0:T(8,128)} %get-tuple-element.16.txt_in), custom_call_target="tpu_custom_call" | custom-call | tf_op jit(solution)/shard_map/place/pallas_call | solution.py:717
